TPU v7x, 128 devices: a whole 4x4x4 slice. The times are simulated.
128 devices in a mesh: role: 2 (over core), shard: 64 (over y, z, x).
Axes of the slice: x: 4, y: 4, z: 4, core: 2. Of those that a mesh axis runs over, the one named last changes fastest.
Arguments:
- history: bfloat16 [1024, 2560, 128], P(None, ('role', 'shard')), may hold values from -20 to 20
- event_cat: int32 [1024, 2560], P(None, ('role', 'shard')), may hold values from 0 to 1023, as said below
- candidates: bfloat16 [1024, 200, 128], P(('role', 'shard')), may hold values from -9 to 9
- cand_cat: int32 [1024, 200], P(('role', 'shard')), may hold values from 0 to 1023, as said below
- w_input: bfloat16 [256, 512], replicated, may hold values from -0.375 to 0.375
- w_output: bfloat16 [512, 128], replicated, may hold values from -0.25 to 0.25
Outputs:
- interest_features: bfloat16 [1024, 200, 128], P(('role', 'shard'))
Inputs may be any that keep to these rules, and one draw needn't show every extreme that they name: `event_cat`: in each aligned block of 20 events of one user, at most 8 events have a category that some candidate of that user has; users 2 i and 2 i + 1 have exactly 8 such events together in every block; every user has a block with exactly 8. `cand_cat`: the candidates of one user carry at most 8 distinct categories.
All inputs are finite; a program needn't handle non-finite values.
Results may differ from a plain program's by a relative error of at most 0.0095.
Values may be sent and summed in bfloat16 or wider, within the bound.
A program may use at most 64 MiB of HBM per device.

v0:
```python
import math

import jax
import jax.numpy as jnp
from jax import lax
from jax.sharding import Mesh
from jax.sharding import PartitionSpec as P

HEADS = 4
QCAT = 8
CAP = 8
ROLE_SHARD = ("role", "shard_0", "shard_1", "shard_2")


def laid_out(pieces, dim):
    pieces = jnp.moveaxis(pieces, 0, dim)
    lengths = pieces.shape
    return pieces.reshape(*lengths[:dim], lengths[dim] * lengths[dim + 1], *lengths[dim + 2 :])


def stacked_from(value, axes, order):
    pieces = value
    for k in order:
        pieces = lax.all_gather(pieces, axes[k])
    done = order[::-1]
    back = [done.index(k) for k in range(len(axes))]
    pieces = pieces.transpose(*back, *range(len(axes), pieces.ndim))
    return pieces.reshape(-1, *value.shape)


def gathered_by_axis(value, axes, order, dim):
    return laid_out(stacked_from(value, axes, order), dim)


def distinct_ids(categories):
    length = categories.shape[1]
    equal_pairs = categories[:, :, None] == categories[:, None, :]
    earlier = jnp.arange(length)[:, None] < jnp.arange(length)[None, :]
    first_seen = jnp.logical_not(jnp.any(equal_pairs & earlier[None, :, :], axis=1))
    seen_rank = jnp.cumsum(first_seen.astype(jnp.int32), axis=1) - 1
    chosen_slot = first_seen[:, :, None] & (
        seen_rank[:, :, None] == jnp.arange(QCAT, dtype=jnp.int32)[None, None, :]
    )
    values = jnp.sum(jnp.where(chosen_slot, categories[:, :, None], 0), axis=1)
    present = jnp.any(chosen_slot, axis=1)
    return jnp.where(present, values, -1)


def attend(queries, event_keys, allowed):
    group = queries.shape[0]
    count = queries.shape[1]
    width = queries.shape[2]
    head_size = width // HEADS
    query_heads = queries.reshape(group, count, HEADS, head_size)
    key_heads = event_keys.reshape(group, -1, HEADS, head_size)
    scores = jnp.einsum(
        "gchk,gshk->ghcs", query_heads, key_heads, preferred_element_type=jnp.float32
    ) * head_size ** (-0.5)
    scores = jnp.where(allowed[:, None, None, :], scores, -1e30)
    row_max = jnp.max(scores, axis=-1, keepdims=True)
    expo = jnp.exp(scores - row_max)
    total = jnp.sum(expo, axis=-1, keepdims=True)
    weights = (expo / total).astype(jnp.bfloat16)
    interest = jnp.einsum("ghcs,gshk->gchk", weights, key_heads, preferred_element_type=jnp.float32)
    return interest.reshape(group, count, width).astype(jnp.bfloat16)


def local(history, event_cat, candidates, cand_cat, w_input, w_output):
    wanted = gathered_by_axis(distinct_ids(cand_cat), ROLE_SHARD, (1, 2, 3, 0), 0)
    hits = jnp.any(event_cat[:, :, None] == wanted[:, None, :], axis=-1)
    slot_rank = jnp.cumsum(hits.astype(jnp.int32), axis=1) - 1
    places = jnp.arange(CAP, dtype=jnp.int32)
    place_values = places.astype(jnp.float32)
    own_users = candidates.shape[0]
    cand_count = candidates.shape[1]
    width = candidates.shape[2]
    rows = own_users * cand_count
    cand_part = jnp.dot(
        candidates.reshape(rows, width), w_input[:width], preferred_element_type=jnp.float32
    )
    hit_counts = jnp.sum(hits.astype(jnp.int32), axis=1)
    pair_counts = hit_counts.reshape(-1, 2)
    start = jnp.stack([jnp.zeros_like(pair_counts[:, 0]), pair_counts[:, 0]], axis=1).reshape(-1)
    shifted = slot_rank + start[:, None]
    selector = (hits[:, None, :] & (shifted[:, None, :] == places[None, :, None])).astype(
        jnp.bfloat16
    )
    spread = jnp.einsum("use,ued->usd", selector, history, preferred_element_type=jnp.float32)
    packed = jnp.sum(spread.reshape(-1, 2, CAP, width), axis=1).astype(jnp.bfloat16)
    received, counts_in = (
        lax.all_to_all(packed, ROLE_SHARD, split_axis=0, concat_axis=1, tiled=True),
        lax.all_to_all(
            pair_counts.astype(jnp.bfloat16), ROLE_SHARD, split_axis=0, concat_axis=1, tiled=True
        ),
    )
    half = own_users // 2
    counts_in = counts_in.astype(jnp.float32).reshape(half, -1, 2)
    lead = counts_in[:, :, 0][:, :, None]
    follow = counts_in[:, :, 1][:, :, None]
    lead_use = place_values[None, None, :] < lead
    follow_use = (place_values[None, None, :] >= lead) & (
        place_values[None, None, :] < lead + follow
    )
    usable = jnp.stack([lead_use, follow_use], axis=1).reshape(own_users, -1)
    received = jnp.repeat(received, 2, axis=0)
    group = math.gcd(own_users, 4)
    packs = own_users // group

    def one_pack(pieces):
        return attend(pieces[0], pieces[1], pieces[2])

    interest = lax.map(
        one_pack,
        (
            candidates.reshape(packs, group, cand_count, width),
            received.reshape(packs, group, -1, width),
            usable.reshape(packs, group, -1),
        ),
    )
    interest = interest.reshape(rows, width)
    hidden = cand_part + jnp.dot(interest, w_input[width:], preferred_element_type=jnp.float32)
    hidden = jax.nn.silu(hidden).astype(jnp.bfloat16)
    result = jnp.dot(hidden, w_output, preferred_element_type=jnp.float32).astype(jnp.bfloat16)
    return result.reshape(own_users, cand_count, width)


def solution(mesh):
    torus = Mesh(
        mesh.devices.reshape(mesh.shape["role"], 4, 4, 4), ("role", "shard_0", "shard_1", "shard_2")
    )
    return jax.shard_map(
        local,
        mesh=torus,
        in_specs=(
            P(None, ROLE_SHARD, None),
            P(None, ROLE_SHARD),
            P(ROLE_SHARD, None, None),
            P(ROLE_SHARD, None),
            P(),
            P(),
        ),
        out_specs=P(ROLE_SHARD, None, None),
        check_vma=False,
    )
```

profile of v0, /device:TPU:1, one launch (start us, length us, event | category | flops | bytes accessed | tf_op | source)
XLA Modules:
  0.0 135.8 jit_solution(7698522752278999011)
XLA Ops:
  0.0 0.0 copy-start
  0.0 1.1 and_reduce_fusion
  1.2 0.6 reduce-window.6
  1.7 0.2 slice_reduce_fusion
  2.0 0.1 add_bitcast_fusion
  2.1 0.9 select_reduce_fusion
  3.0 0.2 fusion.26
  3.2 10.5 %all-gather = s32[32,8]{1,0:T(8,128)S(1)} all-gather(s32[8,8]{1,0:T(8,128)S(1)} %broadcast_select_fusion), channel_id=2, replica_groups=mesh['role'=2,'shard_0'=4,'shard_1'=4,'shard_2'=4] {'shard_0'}, dimensions={0}, use_global_device_ids=true | all-gather | bytes 1280 | tf_op jit(solution)/shard_map/all_gather | solution.py:24
  13.7 10.2 %all-gather.1 = s32[16,8,8]{2,1,0:T(8,128)S(1)} all-gather(s32[4,8,8]{2,1,0:T(8,128)S(1)} %bitcast.74), channel_id=3, replica_groups=mesh['role'=2,'shard_0'=4,'shard_1'=4,'shard_2'=4] {'shard_1'}, dimensions={0}, use_global_device_ids=true | all-gather | bytes 5120 | tf_op jit(solution)/shard_map/all_gather | solution.py:24
  23.9 9.8 %all-gather.2 = s32[16,4,8,8]{3,2,1,0:T(8,128)S(1)} all-gather(s32[4,4,8,8]{3,2,1,0:T(8,128)S(1)} %bitcast.73), channel_id=4, replica_groups=mesh['role'=2,'shard_0'=4,'shard_1'=4,'shard_2'=4] {'shard_2'}, dimensions={0}, use_global_device_ids=true | all-gather | bytes 20480 | tf_op jit(solution)/shard_map/all_gather | solution.py:24
  33.7 11.0 %all-gather.3 = s32[8,4,4,8,8]{4,3,2,1,0:T(8,128)S(1)} all-gather(s32[4,4,4,8,8]{4,3,2,1,0:T(8,128)S(1)} %bitcast.71), channel_id=5, replica_groups=mesh['role'=2,'shard_0'=4,'shard_1'=4,'shard_2'=4] {'role'}, dimensions={0}, use_global_device_ids=true | all-gather | bytes 49152 | tf_op jit(solution)/shard_map/all_gather | solution.py:24
  44.7 0.6 copy.48
  45.3 0.5 eq.61
  45.8 1.1 compare_reduce_fusion
  47.0 0.3 convert_element_type.67
  47.2 1.5 %copy.54 = bf16[128,4,2]{1,2,0:T(2,128)(2,1)} copy(bf16[128,4,2]{2,1,0:T(4,128)(2,1)S(1)} %convert_element_type.67) | data formatting | bytes 4096 | tf_op jit(solution)/shard_map/convert_element_type | solution.py:93
  48.8 7.8 %all-to-all-start.1 = ((bf16[128,4,2]{1,2,0:T(2,128)(2,1)}), bf16[128,4,2]{1,2,0:T(2,128)(2,1)S(1)}, u32[]{:S(2)}, u32[]{:S(2)}) async-start(bf16[128,4,2]{1,2,0:T(2,128)(2,1)} %copy.54), calls=%async_computation.1 | async-start | bytes 131072 | tf_op jit(solution)/shard_map/all_to_all | solution.py:92
  56.6 0.2 reshape.136
  56.8 0.3 copy.49
  57.1 0.1 stack.8
  57.2 0.2 add.35
  57.4 0.1 reduce_window_sum.28
  57.5 0.2 copy.50
  57.7 0.0 copy-start.1
  57.8 0.0 copy-start.2
  57.8 8.8 %bitcast_reduce_fusion = bf16[512,8,128]{2,1,0:T(8,128)(2,1)} fusion(bf16[1024,20,128]{2,0,1:T(8,128)(2,1)} %param.8, s32[1024,20]{1,0:T(8,128)S(1)} %copy.50, pred[1024,20]{1,0:T(8,128)(4,1)S(1)} %copy.49), kind=kOutput, calls=%fused_computation.19 | convolution fusion | flops 42795008 | bytes 6393856 | tf_op jit(solution)/shard_map/use,ued->usd/dot_general | solution.py:88
  66.6 0.0 copy-done.1
  66.6 1.0 copy.58
  67.6 0.0 all-to-all-done.1
  67.6 9.8 %all-to-all-start = ((bf16[512,8,128]{2,1,0:T(8,128)(2,1)}), bf16[512,8,128]{2,1,0:T(8,128)(2,1)S(1)}, u32[]{:S(2)}, u32[]{:S(2)}) async-start(bf16[512,8,128]{2,1,0:T(8,128)(2,1)} %bitcast_reduce_fusion), calls=%async_computation | async-start | bytes 2097152 | tf_op jit(solution)/shard_map/all_to_all | solution.py:91
  77.4 0.0 copy-done.2
  77.4 2.2 %fusion.23 = f32[1600,512]{1,0:T(8,128)} fusion(bf16[1600,128]{1,0:T(8,128)(2,1)S(1)} %bitcast.70, bf16[256,512]{1,0:T(8,128)(2,1)S(1)} %copy-done.2), kind=kOutput, calls=%fused_computation.33 | convolution fusion | flops 209715200 | bytes 3817472 | tf_op jit(solution)/shard_map/dot_general | solution.py:78
  79.7 0.1 fusion.29
  79.8 0.1 copy.55
  79.9 0.1 copy.56
  79.9 0.1 broadcast_compare_fusion
  80.0 0.3 copy.57
  80.3 0.3 reshape_reshape.7
  80.6 15.4 %all-to-all-done = bf16[512,8,128]{2,1,0:T(8,128)(2,1)S(1)} async-done(((bf16[512,8,128]{2,1,0:T(8,128)(2,1)}), bf16[512,8,128]{2,1,0:T(8,128)(2,1)S(1)}, u32[]{:S(2)}, u32[]{:S(2)}) %all-to-all-start) | async-done | bytes 1048608 | tf_op jit(solution)/shard_map/all_to_all | solution.py:91
  96.1 0.2 copy.67
  96.3 0.5 copy.53
  96.8 0.3 broadcast_in_dim.39
  97.0 34.5 %while.10 = (s32[]{:T(128)}, bf16[2,4,200,128]{3,2,1,0:T(8,128)(2,1)}, bf16[2,4,1024,128]{2,3,1,0:T(8,128)(2,1)S(1)}, pred[2,4,1024]{2,1,0:T(4,128)(4,1)S(1)}, bf16[2,4,200,128]{2,3,1,0:T(8,128)(2,1)}, /*index=5*/s32[]{:T(128)}) while((s32[]{:T(128)}, bf16[2,4,200,128]{3,2,1,0:T(8,128)(2,1)}, bf16[2,4,1024,128]{2,3,1,0:T(8,128)(2,1)S(1)}, ...), condition=%wide.region_12.13_spmd, body=%wide.region_9.12_spmd.sunk | while | flops 439194624 | bytes 32085584 | solution.py:112
  97.1 0.1 constant_dynamic-slice_fusion.4
  97.1 1.0 constant_dynamic-slice_fusion.5
  98.1 8.3 %fusion.46 = (f32[4,4,200]{2,1,0:T(4,128)}, f32[4,4,200,1024]{3,2,1,0:T(8,128)}) fusion(pred[4,1024]{1,0:T(4,128)(4,1)S(1)} %dynamic-slice_bitcast_fusion.2, bf16[4,200,4,32]{1,3,2,0:T(8,128)(2,1)S(1)} %bitcast.64, bf16[4,1024,4,32]{1,3,2,0:T(8,128)(2,1)S(1)} %bitcast.61), kind=kOutput, calls=%fused_computation.52.clone.1 | convolution fusion | flops 222823424 | bytes 14377472 | tf_op jit(solution)/shard_map/while/body/eval_jaxpr/sub | solution.py:61
  106.4 7.0 %fusion.47 = bf16[4,4,32,200]{3,2,1,0:T(8,128)(2,1)S(1)} fusion(bf16[4,1024,4,32]{1,3,2,0:T(8,128)(2,1)S(1)} %bitcast.62, f32[4,4,200,1024]{3,2,1,0:T(8,128)} %get-tuple-element.82, f32[4,4,200]{2,1,0:T(4,128)} %get-tuple-element.83), kind=kOutput, calls=%fused_computation.10.clone.1 | convolution fusion | flops 216371200 | bytes 14373376 | tf_op jit(solution)/shard_map/while/body/eval_jaxpr/ghcs,gshk->gchk/dot_general | solution.py:64
  113.4 0.2 copy.69
  113.6 0.7 constant_dynamic-update-slice_fusion.2
  114.3 0.1 constant_dynamic-slice_fusion.4
  114.4 1.0 constant_dynamic-slice_fusion.5
  115.4 8.3 %fusion.46 = (f32[4,4,200]{2,1,0:T(4,128)}, f32[4,4,200,1024]{3,2,1,0:T(8,128)}) fusion(pred[4,1024]{1,0:T(4,128)(4,1)S(1)} %dynamic-slice_bitcast_fusion.2, bf16[4,200,4,32]{1,3,2,0:T(8,128)(2,1)S(1)} %bitcast.64, bf16[4,1024,4,32]{1,3,2,0:T(8,128)(2,1)S(1)} %bitcast.61), kind=kOutput, calls=%fused_computation.52.clone.1 | convolution fusion | flops 222823424 | bytes 14377472 | tf_op jit(solution)/shard_map/while/body/eval_jaxpr/sub | solution.py:61
  123.6 7.0 %fusion.47 = bf16[4,4,32,200]{3,2,1,0:T(8,128)(2,1)S(1)} fusion(bf16[4,1024,4,32]{1,3,2,0:T(8,128)(2,1)S(1)} %bitcast.62, f32[4,4,200,1024]{3,2,1,0:T(8,128)} %get-tuple-element.82, f32[4,4,200]{2,1,0:T(4,128)} %get-tuple-element.83), kind=kOutput, calls=%fused_computation.10.clone.1 | convolution fusion | flops 216371200 | bytes 14373376 | tf_op jit(solution)/shard_map/while/body/eval_jaxpr/ghcs,gshk->gchk/dot_general | solution.py:64
  130.6 0.2 copy.69
  130.8 0.7 constant_dynamic-update-slice_fusion.2
  131.5 0.0 copy-done
  131.5 4.3 %convolution_convert_fusion = bf16[1600,128]{1,0:T(8,128)(2,1)} fusion(bf16[512,128]{1,0:T(8,128)(2,1)S(1)} %copy-done, f32[1600,512]{1,0:T(8,128)} %fusion.23, bf16[1600,128]{1,0:T(8,128)(2,1)} %bitcast.77, bf16[256,512]{1,0:T(8,128)(2,1)} %param.12), kind=kOutput, calls=%fused_computation.24 | convolution fusion | flops 424550400 | bytes 4358144 | tf_op jit(solution)/shard_map/dot_general | solution.py:123
  (17 shorter events, 0.2 us)
Async XLA Ops:
  0.0 131.5 %copy-start = (bf16[512,128]{1,0:T(8,128)(2,1)S(1)}, bf16[512,128]{1,0:T(8,128)(2,1)}, u32[]{:S(2)}) copy-start(bf16[512,128]{1,0:T(8,128)(2,1)} %param.13) | copy-start | bytes 393220
  48.8 18.9 %all-to-all-start.1 = ((bf16[128,4,2]{1,2,0:T(2,128)(2,1)}), bf16[128,4,2]{1,2,0:T(2,128)(2,1)S(1)}, u32[]{:S(2)}, u32[]{:S(2)}) async-start(bf16[128,4,2]{1,2,0:T(2,128)(2,1)} %copy.54), calls=%async_computation.1 | async-start | bytes 131072 | tf_op jit(solution)/shard_map/all_to_all | solution.py:92
  57.7 8.8 %copy-start.1 = (bf16[8,200,128]{2,1,0:T(8,128)(2,1)S(1)}, bf16[8,200,128]{2,1,0:T(8,128)(2,1)}, u32[]{:S(2)}) copy-start(bf16[8,200,128]{2,1,0:T(8,128)(2,1)} %param.10) | copy-start | bytes 1228804
  57.8 19.6 %copy-start.2 = (bf16[256,512]{1,0:T(8,128)(2,1)S(1)}, bf16[256,512]{1,0:T(8,128)(2,1)}, u32[]{:S(2)}) copy-start(bf16[256,512]{1,0:T(8,128)(2,1)} %param.12) | copy-start | bytes 786436
  67.6 28.4 %all-to-all-start = ((bf16[512,8,128]{2,1,0:T(8,128)(2,1)}), bf16[512,8,128]{2,1,0:T(8,128)(2,1)S(1)}, u32[]{:S(2)}, u32[]{:S(2)}) async-start(bf16[512,8,128]{2,1,0:T(8,128)(2,1)} %bitcast_reduce_fusion), calls=%async_computation | async-start | bytes 2097152 | tf_op jit(solution)/shard_map/all_to_all | solution.py:91
where the time goes:
time: 136 us
  matrix products  45.8 us (34%)
  blocking collectives  41.5 us (31%)
  starting transfers between devices  17.6 us (13%)
  waiting for transfers between devices  15.5 us (11%)
  local copies, waits for them, and re-layouts  10.6 us (8%)
  other arithmetic  4.5 us (3%)
    all_gather x4, blocking collectives, stacked_from(): pieces = lax.all_gather(pieces, axes[k])  41.5 us
    sub x2, matrix products, attend(): expo = jnp.exp(scores - row_max)  16.5 us
    all_to_all x1, waiting for transfers between devices, local(): lax.all_to_all(packed, ROLE_SHARD, split_axis=0, concat_axis=1, tiled=True)  15.4 us
    dot_general x2, matrix products, attend(): jnp.einsum('ghcs,gshk->gchk', weights, key_heads, preferred_element_type=...  14 us
    all_to_all x1, starting transfers between devices, local(): lax.all_to_all(packed, ROLE_SHARD, split_axis=0, concat_axis=1, tiled=True)  9.77 us
    dot_general x1, matrix products, local(): jnp.einsum('use,ued->usd', selector, history, preferred_element_type=jnp....  8.81 us
    all_to_all x1, starting transfers between devices, local(): lax.all_to_all(pair_counts.astype(jnp.bfloat16), ROLE_SHARD, split_axis=0...  7.84 us
    dot_general x1, matrix products, local(): jnp.dot(hidden, w_output, preferred_element_type=jnp.float32)  4.26 us
  transfers between devices with their start and end apart: 2, of which 1 were waited for; matrix products, arithmetic and copies ran while one was open for 10% of the time, Pallas kernels for 0%

commit v1 on v0

v1 whole, which is shorter than its diff:
```python
import functools
import jax
import jax.numpy as jnp
from jax import lax
from jax.experimental import pallas as pl
from jax.experimental.pallas import tpu as pltpu
from jax.sharding import PartitionSpec as P

AXES = ("role", "shard")
MESH = pl.DeviceIdType.MESH
DEVS = 128
SIDE = 4
E_DEV = 20
QCAT = 8
CAP = 8
OWN = 8
PAIRS = OWN // 2
LANES = E_DEV * OWN
WIDTH = 128


def partner(i, role, y, z, x):
    r = lax.rem(role + lax.rem(i, 2), 2)
    j = i // 2
    px = lax.rem(x + lax.rem(j, 4), 4)
    pz = lax.rem(z + lax.rem(j // 4, 4), 4)
    py = lax.rem(y + j // 16, 4)
    return r, py * 16 + pz * 4 + px


def exchange_kernel(hist_hbm, cats_ref, cand_cat_ref, recv_ref, cnt_in_ref,
                    hist_ref, id_row_ref, ids_ref, key_ref, cnt_ref, send_ref,
                    hist_sems, id_send, id_recv, cnt_send, cnt_recv, data_send, data_recv):
    role = lax.axis_index("role")
    shard = lax.axis_index("shard")
    y, z, x = shard // 16, lax.rem(shard // 4, 4), lax.rem(shard, 4)
    me = role * 64 + shard

    barrier = pltpu.get_barrier_semaphore()

    def greet(i, carry):
        r, s = partner(i, role, y, z, x)
        pl.semaphore_signal(barrier, inc=1, device_id={"role": r, "shard": s}, device_id_type=MESH)
        return carry

    lax.fori_loop(1, DEVS, greet, 0)

    loads = [
        pltpu.make_async_copy(hist_hbm.at[e], hist_ref.at[:, pl.ds(e * OWN, OWN), :], hist_sems.at[e])
        for e in range(E_DEV)
    ]
    for load in loads:
        load.start()

    cats = cand_cat_ref[...].astype(jnp.float32)
    lane = lax.broadcasted_iota(jnp.int32, (OWN, WIDTH), 1)
    sub = lax.broadcasted_iota(jnp.int32, (OWN, WIDTH), 0)
    spread = jnp.zeros((OWN, WIDTH), jnp.float32)
    last = jnp.full((OWN, 1), -1.0, jnp.float32)
    for k in range(QCAT):
        last = jnp.min(jnp.where(cats > last, cats, 4096.0), axis=1, keepdims=True)
        spot = (lax.rem(lane, 8) == sub) & (lax.rem(lane // 8, 8) == k)
        spread = jnp.where(spot, last, spread)
    row = jnp.sum(spread, axis=0, keepdims=True).astype(jnp.int32)
    low = lax.rem(row, 32)
    lane1 = lax.broadcasted_iota(jnp.int32, (1, WIDTH), 1)
    id_row_ref[...] = jnp.where(lane1 < 64, row - low, low).astype(jnp.float32)

    pl.semaphore_wait(barrier, DEVS - 1)

    def send_ids(i, carry):
        r, s = partner(i, role, y, z, x)
        pltpu.make_async_remote_copy(
            src_ref=id_row_ref, dst_ref=ids_ref.at[pl.ds(me, 1)],
            send_sem=id_send, recv_sem=id_recv,
            device_id={"role": r, "shard": s}, device_id_type=MESH).start()
        return carry

    lax.fori_loop(1, DEVS, send_ids, 0)
    pltpu.make_async_copy(id_row_ref, ids_ref.at[pl.ds(me, 1)], id_recv).start()
    pltpu.make_async_copy(ids_ref, ids_ref, id_recv).wait()

    ids = ids_ref[...].astype(jnp.bfloat16)
    lane_i = lax.broadcasted_iota(jnp.int32, (DEVS, WIDTH), 1)
    stacked = jnp.concatenate(
        [jnp.where(lax.rem(lane_i // 8, 8) == k, ids, jnp.zeros_like(ids)) for k in range(QCAT)], axis=0)
    er = lax.broadcasted_iota(jnp.int32, (WIDTH, LANES), 0)
    ec = lax.broadcasted_iota(jnp.int32, (WIDTH, LANES), 1)
    expand = jnp.where(lax.rem(er, 8) == lax.rem(ec, 8), 1.0, 0.0).astype(jnp.bfloat16)
    wanted = jnp.dot(stacked, expand, preferred_element_type=jnp.float32)
    events = cats_ref[...]
    hit = events == wanted[0:DEVS]
    for k in range(1, QCAT):
        hit = hit | (events == wanted[k * DEVS:(k + 1) * DEVS])
    hits = jnp.where(hit, 1.0, 0.0).astype(jnp.bfloat16)
    a = lax.broadcasted_iota(jnp.int32, (LANES, LANES), 0)
    b = lax.broadcasted_iota(jnp.int32, (LANES, LANES), 1)
    ua, ub = lax.rem(a, 8), lax.rem(b, 8)
    before = ((ua == ub) & (a < b)) | ((ua + 1 == ub) & (lax.rem(ub, 2) == 1))
    rank = jnp.dot(hits, jnp.where(before, 1.0, 0.0).astype(jnp.bfloat16), preferred_element_type=jnp.float32)
    lane_k = lax.broadcasted_iota(jnp.int32, (DEVS, LANES), 1)
    base = (lax.rem(lane_k, 8) // 2 * CAP).astype(jnp.float32)
    key_ref[...] = jnp.where(hit, base + rank, -1.0)
    ca = lax.broadcasted_iota(jnp.int32, (LANES, WIDTH), 0)
    cb = lax.broadcasted_iota(jnp.int32, (LANES, WIDTH), 1)
    lead_of = jnp.where(lax.rem(ca, 8) == cb // 8 * 2, 1.0, 0.0).astype(jnp.bfloat16)
    cnt_ref[...] = jnp.dot(hits, lead_of, preferred_element_type=jnp.float32)

    for load in loads:
        load.wait()

    rows = lax.broadcasted_iota(jnp.int32, (PAIRS * CAP, LANES), 0).astype(jnp.float32)

    def fill(i):
        r, s = partner(i, role, y, z, x)
        t = r * 64 + s
        pick = jnp.where(key_ref[pl.ds(t, 1), :] == rows, 1.0, 0.0).astype(jnp.bfloat16)
        packed = jnp.dot(pick, hist_ref[t], preferred_element_type=jnp.float32)
        send_ref[i] = packed.astype(jnp.bfloat16).reshape(PAIRS, CAP, WIDTH)
        return r, s, t

    def data_step(i, carry):
        r, s, t = fill(i)
        pltpu.make_async_remote_copy(
            src_ref=cnt_ref.at[pl.ds(t, 1)], dst_ref=cnt_in_ref.at[pl.ds(me, 1)],
            send_sem=cnt_send, recv_sem=cnt_recv,
            device_id={"role": r, "shard": s}, device_id_type=MESH).start()
        pltpu.make_async_remote_copy(
            src_ref=send_ref.at[i], dst_ref=recv_ref.at[:, me],
            send_sem=data_send, recv_sem=data_recv,
            device_id={"role": r, "shard": s}, device_id_type=MESH).start()
        return carry

    lax.fori_loop(1, DEVS, data_step, 0)
    fill(0)
    pltpu.make_async_copy(send_ref.at[0], recv_ref.at[:, me], data_recv).start()
    pltpu.make_async_copy(cnt_ref.at[pl.ds(me, 1)], cnt_in_ref.at[pl.ds(me, 1)], cnt_recv).start()
    pltpu.make_async_copy(recv_ref, recv_ref, data_recv).wait()
    pltpu.make_async_copy(cnt_in_ref, cnt_in_ref, cnt_recv).wait()
    others = pl.ds(0, DEVS - 1)
    pltpu.make_async_copy(send_ref.at[others], send_ref.at[others], data_send).wait()
    pltpu.make_async_copy(cnt_ref.at[others], cnt_ref.at[others], cnt_send).wait()
    pltpu.make_async_copy(ids_ref.at[others], ids_ref.at[others], id_send).wait()


def exchange(history, event_cat, cand_cat):
    hist = history.transpose(1, 0, 2).reshape(E_DEV, DEVS, OWN, WIDTH)
    cats = event_cat.astype(jnp.float32).T.reshape(E_DEV, DEVS, OWN).transpose(1, 0, 2).reshape(DEVS, LANES)
    vm = pl.BlockSpec(memory_space=pltpu.VMEM)
    return pl.pallas_call(
        exchange_kernel,
        out_shape=(jax.ShapeDtypeStruct((PAIRS, DEVS, CAP, WIDTH), jnp.bfloat16),
                   jax.ShapeDtypeStruct((DEVS, WIDTH), jnp.float32)),
        in_specs=[pl.BlockSpec(memory_space=pl.ANY), vm, vm],
        out_specs=(vm, vm),
        scratch_shapes=[
            pltpu.VMEM((DEVS, LANES, WIDTH), jnp.bfloat16),
            pltpu.VMEM((1, WIDTH), jnp.float32),
            pltpu.VMEM((DEVS, WIDTH), jnp.float32),
            pltpu.VMEM((DEVS, LANES), jnp.float32),
            pltpu.VMEM((DEVS, WIDTH), jnp.float32),
            pltpu.VMEM((DEVS, PAIRS, CAP, WIDTH), jnp.bfloat16),
            pltpu.SemaphoreType.DMA((E_DEV,)),
        ] + [pltpu.SemaphoreType.DMA] * 6,
        compiler_params=pltpu.CompilerParams(collective_id=0, has_side_effects=True,
                                             vmem_limit_bytes=60 << 20),
        name="exchange",
    )(hist, cats, cand_cat)


def head_attention(history_slots, lead, candidates, w_input, w_output):
    own = candidates.shape[0]
    slots = history_slots.reshape(PAIRS, DEVS * CAP, WIDTH)
    counts = lead[:, :PAIRS * CAP].T.reshape(PAIRS, CAP, DEVS).transpose(0, 2, 1)
    is_lead = (jnp.arange(CAP, dtype=jnp.float32)[None, None, :] < counts).reshape(PAIRS, DEVS * CAP)
    usable = jnp.stack([is_lead, ~is_lead], axis=1).reshape(own, DEVS * CAP)
    keys = jnp.repeat(slots, 2, axis=0).reshape(own, DEVS * CAP, 4, 32)
    q = candidates.reshape(own, -1, 4, 32)
    s = jnp.einsum("gchk,gshk->ghcs", q, keys, preferred_element_type=jnp.float32) * 32 ** -0.5
    s = jnp.where(usable[:, None, None, :], s, -1e30)
    e = jnp.exp(s - jnp.max(s, axis=-1, keepdims=True))
    w = (e / jnp.sum(e, axis=-1, keepdims=True)).astype(jnp.bfloat16)
    interest = jnp.einsum("ghcs,gshk->gchk", w, keys, preferred_element_type=jnp.float32)
    interest = interest.reshape(own, -1, WIDTH).astype(jnp.bfloat16)
    rows = jnp.concatenate([candidates, interest], axis=-1)
    hidden = jax.nn.silu(jnp.einsum("gck,kn->gcn", rows, w_input, preferred_element_type=jnp.float32)).astype(jnp.bfloat16)
    return jnp.einsum("gcn,nd->gcd", hidden, w_output, preferred_element_type=jnp.float32).astype(jnp.bfloat16)


def local(history, event_cat, candidates, cand_cat, w_input, w_output):
    slots, lead = exchange(history, event_cat, cand_cat)
    return head_attention(slots, lead, candidates, w_input, w_output)


def solution(mesh):
    return jax.shard_map(
        local, mesh=mesh,
        in_specs=(P(None, AXES, None), P(None, AXES), P(AXES, None, None), P(AXES, None), P(), P()),
        out_specs=P(AXES, None, None), check_vma=False)
```

time: 136 us -> 83.2 us (0.61)
  Pallas kernels: 0 us -> 47.5 us
  blocking collectives: 41.5 us -> 0 us
  matrix products: 45.8 us -> 27.7 us
  starting transfers between devices: 17.6 us -> 0 us
  waiting for transfers between devices: 15.5 us -> 0 us
  local copies, waits for them, and re-layouts: 10.6 us -> 6.55 us
  other arithmetic: 4.5 us -> 0.99 us
    pallas_call x0 -> x1, Pallas kernels: none -> 47.5 us  [exchange(): pl.pallas_call(exchange_kernel, out_shape=(jax.ShapeDtypeStruct((PAIRS, D...]
    all_gather x4 -> x0, blocking collectives: 41.5 us -> none  [stacked_from(): pieces = lax.all_gather(pieces, axes[k])]
    all_to_all x2 -> x0, starting transfers between devices: 17.6 us -> none  [the longest x1 9.77 us: local(): lax.all_to_all(packed, ROLE_SHARD, split_axis=0, concat_axis=1, tiled=True)]
    dot_general x5 -> x2, matrix products: 29.3 us -> 12.7 us  [the longest x1 10.7 us: head_attention(): jnp.einsum('ghcs,gshk->gchk', w, keys, preferred_element_type=jnp.float32)]
    all_to_all x2 -> x0, waiting for transfers between devices: 15.5 us -> none  [the longest x1 15.4 us: local(): lax.all_to_all(packed, ROLE_SHARD, split_axis=0, concat_axis=1, tiled=True)]
    reduce_or x3 -> x0, other arithmetic: 2.44 us -> none  [the longest x1 1.12 us: local(): hits = jnp.any(event_cat[:, :, None] == wanted[:, None, :], axis=-1)]
    dynamic_slice x4 -> x0, local copies, waits for them, and re-layouts: 2.09 us -> none  [local(): lax.map(one_pack, (candidates.reshape(packs, group, cand_count, width), r...]
    reshape x1 -> x2, local copies, waits for them, and re-layouts: 0.2 us -> 2.25 us  [the longest x1 1.49 us: head_attention(): slots = history_slots.reshape(PAIRS, DEVS * CAP, WIDTH)]
  transfers between devices with their start and end apart: 2 -> 0, of which waited for: 1 -> 0; matrix products, arithmetic and copies ran while one was open for 10% -> 0% of each run, Pallas kernels for 0% -> 0%
where the time goes in v1:
time: 83.2 us; the launch traced here: 82.9 us
  Pallas kernels  47.5 us (57%)
  matrix products  27.7 us (33%)
  local copies, waits for them, and re-layouts  6.55 us (8%)
  other arithmetic  0.99 us (1%)
    pallas_call x1, Pallas kernels, exchange(): pl.pallas_call(exchange_kernel, out_shape=(jax.ShapeDtypeStruct((PAIRS, D...  47.5 us
    sub x1, matrix products, head_attention(): e = jnp.exp(s - jnp.max(s, axis=-1, keepdims=True))  15 us
    dot_general x1, matrix products, head_attention(): jnp.einsum('ghcs,gshk->gchk', w, keys, preferred_element_type=jnp.float32)  10.7 us
    unnamed x7, local copies, waits for them, and re-layouts  2.01 us
    dot_general x1, matrix products, head_attention(): jnp.einsum('gcn,nd->gcd', hidden, w_output, preferred_element_type=jnp.fl...  1.92 us

profile of v1, /device:TPU:1, one launch (start us, length us, event | category | flops | bytes accessed | tf_op | source)
XLA Modules:
  0.0 82.9 jit_solution(1479949550809262220)
XLA Ops:
  0.0 0.0 copy-start
  0.0 0.9 %convert_bitcast_fusion = f32[20,1024]{1,0:T(8,128)S(1)} fusion(s32[1024,20]{0,1:T(8,128)} %param.7), kind=kLoop, calls=%fused_computation.21 | loop fusion | flops 20480 | bytes 163840 | tf_op jit(solution)/shard_map/transpose | solution.py:148
  0.9 0.2 copy.11
  1.2 0.2 copy.12
  1.4 0.8 copy.13.cats_ref
  2.2 2.0 %copy.18 = bf16[8,200,128]{1,2,0:T(8,128)(2,1)} copy(bf16[8,200,128]{2,1,0:T(8,128)(2,1)} %param.8) | data formatting | bytes 819200 | tf_op args[2]
  4.2 47.5 %exchange.1 = (bf16[4,128,8,128]{3,2,1,0:T(8,128)(2,1)}, f32[128,128]{1,0:T(8,128)}) custom-call(bf16[20,128,8,128]{3,2,1,0:T(8,128)(2,1)} %bitcast.44, f32[128,160]{1,0:T(8,128)} %copy.13.cats_ref, s32[8,200]{1,0:T(8,128)} %cand_cat_ref.1), custom_call_target="tpu_custom_call" | custom-call | tf_op jit(solution)/shard_map/exchange/pallas_call | solution.py:150
  51.7 1.5 %copy.14 = bf16[4,1024,128]{1,2,0:T(8,128)(2,1)S(1)} copy(bf16[4,1024,128]{2,1,0:T(8,128)(2,1)} %bitcast.48) | data formatting | bytes 2097152 | tf_op jit(solution)/shard_map/reshape | solution.py:173
  53.2 0.8 %slice_bitcast_fusion = f32[32,128]{0,1:T(8,128)S(1)} fusion(f32[128,128]{1,0:T(8,128)} %get-tuple-element.8), kind=kLoop, calls=%fused_computation.22 | loop fusion | bytes 32768 | tf_op jit(solution)/shard_map/transpose | solution.py:174
  54.1 0.1 copy.15
  54.1 0.2 copy.16
  54.3 0.2 stack_reshape.3
  54.6 0.3 broadcast_in_dim.20
  54.9 15.0 %fusion.28 = (f32[8,4,200]{2,1,0:T(4,128)S(1)}, f32[8,4,200,1024]{3,2,1,0:T(8,128)}) fusion(pred[8,1024]{1,0:T(8,128)(4,1)S(1)} %broadcast_in_dim.21, bf16[8,1024,4,32]{1,3,2,0:T(8,128)(2,1)S(1)} %bitcast.45, bf16[8,200,4,32]{1,3,2,0:T(8,128)(2,1)} %bitcast.49), kind=kOutput, calls=%fused_computation.29 | convolution fusion | flops 445645824 | bytes 28754944 | tf_op jit(solution)/shard_map/sub | solution.py:181
  69.9 0.0 copy-start.1
  69.9 0.0 copy-start.2
  69.9 10.7 %fusion.12 = bf16[8,4,32,200]{3,2,1,0:T(8,128)(2,1)S(1)} fusion(bf16[8,1024,4,32]{1,3,2,0:T(8,128)(2,1)S(1)} %bitcast.46, f32[8,4,200,1024]{3,2,1,0:T(8,128)} %get-tuple-element.10, f32[8,4,200]{2,1,0:T(4,128)S(1)} %get-tuple-element.9), kind=kOutput, calls=%fused_computation.14 | convolution fusion | flops 432742400 | bytes 28746752 | tf_op jit(solution)/shard_map/ghcs,gshk->gchk/dot_general | solution.py:183
  80.7 0.3 copy.19
  80.9 0.0 copy-done
  81.0 0.0 copy-done.1
  81.0 0.0 copy-done.2
  81.0 1.9 %fusion.13 = bf16[8,200,128]{2,1,0:T(8,128)(2,1)} fusion(bf16[8,200,128]{2,1,0:T(8,128)(2,1)S(1)} %copy.19, bf16[8,200,128]{2,1,0:T(8,128)(2,1)S(1)} %copy-done.1, bf16[256,512]{1,0:T(8,128)(2,1)S(1)} %copy-done, bf16[512,128]{1,0:T(8,128)(2,1)S(1)} %copy-done.2), kind=kOutput, calls=%fused_computation.15 | convolution fusion | flops 635084800 | bytes 1622016 | tf_op jit(solution)/shard_map/gcn,nd->gcd/dot_general | solution.py:187
  (5 shorter events, 0.1 us)
Async XLA Ops:
  0.0 80.9 %copy-start = (bf16[256,512]{1,0:T(8,128)(2,1)S(1)}, bf16[256,512]{1,0:T(8,128)(2,1)}, u32[]{:S(2)}) copy-start(bf16[256,512]{1,0:T(8,128)(2,1)} %param.10) | copy-start | bytes 786436
  69.9 11.1 %copy-start.1 = (bf16[8,200,128]{2,1,0:T(8,128)(2,1)S(1)}, bf16[8,200,128]{2,1,0:T(8,128)(2,1)}, u32[]{:S(2)}) copy-start(bf16[8,200,128]{2,1,0:T(8,128)(2,1)} %param.8) | copy-start | bytes 1228804
  69.9 11.1 %copy-start.2 = (bf16[512,128]{1,0:T(8,128)(2,1)S(1)}, bf16[512,128]{1,0:T(8,128)(2,1)}, u32[]{:S(2)}) copy-start(bf16[512,128]{1,0:T(8,128)(2,1)} %param.11) | copy-start | bytes 393220

commit v2 on v1

v2 whole, which is shorter than its diff:
```python
import math

import jax
import jax.numpy as jnp
from jax import lax
from jax.experimental import pallas as pl
from jax.experimental.pallas import tpu as pltpu
from jax.sharding import PartitionSpec as P

AXES = ("role", "shard")
MESH = pl.DeviceIdType.MESH
DEVS = 128
SIDE = 4
E_DEV = 20
QCAT = 8
CAP = 8
OWN = 8
PAIRS = OWN // 2
LANES = E_DEV * OWN
WIDTH = 128


CANDS = 200
ROWS = 208
HEADS = 4
CHUNKS = 4
PER_CHUNK = DEVS // CHUNKS
SLOTS = PER_CHUNK * CAP
BLOCK = 16
SCALE = 32 ** -0.5 * math.log2(math.e)
FAR = (2, 3, 1, 0)


def far(k):
    late = k // 2
    return (2 + k) * (1 - late) + (3 - k) * late


def place():
    role = lax.axis_index("role")
    shard = lax.axis_index("shard")
    return role, shard // 16, lax.rem(shard // 4, 4), lax.rem(shard, 4)


def partner(block, k, at):
    role, y, z, x = at
    r = lax.rem(role + 1 - k % 2, 2)
    px = lax.rem(x + FAR[(k // 2) % 4], 4)
    pz = lax.rem(z + far(lax.rem(block, 2) * 2 + k // 8), 4)
    py = lax.rem(y + far(block // 2), 4)
    return r, py * 16 + pz * 4 + px


def signal(sem, r, s):
    pl.semaphore_signal(sem, inc=1, device_id={"role": r, "shard": s}, device_id_type=MESH)


def push(src, dst, send_sem, recv_sem, r, s):
    pltpu.make_async_remote_copy(
        src_ref=src, dst_ref=dst, send_sem=send_sem, recv_sem=recv_sem,
        device_id={"role": r, "shard": s}, device_id_type=MESH).start()


def landed(ref, sem):
    pltpu.make_async_copy(ref, ref, sem).wait()


def line_peers(at):
    role, y, z, x = at
    return [(lax.rem(role + dr, 2), y * 16 + z * 4 + lax.rem(x + dx, 4))
            for dr in range(2) for dx in range(4) if dr or dx]


def plane_peers(at):
    role, y, z, x = at
    return [(role, lax.rem(y + dy, 4) * 16 + lax.rem(z + dz, 4) * 4 + x)
            for dy in FAR for dz in FAR if dy or dz]


def distinct_row(cats):
    lane = lax.broadcasted_iota(jnp.int32, (OWN, WIDTH), 1)
    sub = lax.broadcasted_iota(jnp.int32, (OWN, WIDTH), 0)
    spread = jnp.zeros((OWN, WIDTH), jnp.float32)
    last = jnp.full((OWN, 1), -1.0, jnp.float32)
    for k in range(QCAT):
        last = jnp.min(jnp.where(cats > last, cats, 4096.0), axis=1, keepdims=True)
        spot = (lax.rem(lane, 8) == sub) & (lax.rem(lane // 8, 8) == k)
        spread = jnp.where(spot, last, spread)
    row = jnp.sum(spread, axis=0, keepdims=True).astype(jnp.int32)
    low = lax.rem(row, 32)
    lane1 = lax.broadcasted_iota(jnp.int32, (1, WIDTH), 1)
    return jnp.where(lane1 < 64, row - low, low).astype(jnp.float32)


def matched(ids, events):
    ids = ids.astype(jnp.bfloat16)
    lane_i = lax.broadcasted_iota(jnp.int32, (DEVS, WIDTH), 1)
    er = lax.broadcasted_iota(jnp.int32, (WIDTH, LANES), 0)
    ec = lax.broadcasted_iota(jnp.int32, (WIDTH, LANES), 1)
    expand = jnp.where(lax.rem(er, 8) == lax.rem(ec, 8), 1.0, 0.0).astype(jnp.bfloat16)
    hit = None
    for k in range(QCAT):
        only = jnp.where(lax.rem(lane_i // 8, 8) == k, ids, jnp.zeros_like(ids))
        same = events == jnp.dot(only, expand, preferred_element_type=jnp.float32)
        hit = same if hit is None else hit | same
    hits = jnp.where(hit, 1.0, 0.0).astype(jnp.bfloat16)
    a = lax.broadcasted_iota(jnp.int32, (LANES, LANES), 0)
    b = lax.broadcasted_iota(jnp.int32, (LANES, LANES), 1)
    ua, ub = lax.rem(a, 8), lax.rem(b, 8)
    before = ((ua == ub) & (a < b)) | ((ua + 1 == ub) & (lax.rem(ub, 2) == 1))
    rank = jnp.dot(hits, jnp.where(before, 1.0, 0.0).astype(jnp.bfloat16), preferred_element_type=jnp.float32)
    lane_k = lax.broadcasted_iota(jnp.int32, (DEVS, LANES), 1)
    base = (lax.rem(lane_k, 8) // 2 * CAP).astype(jnp.float32)
    ca = lax.broadcasted_iota(jnp.int32, (LANES, WIDTH), 0)
    cb = lax.broadcasted_iota(jnp.int32, (LANES, WIDTH), 1)
    lead_of = jnp.where(lax.rem(ca, 8) == cb // 32 * 2, 1.0, 0.0).astype(jnp.bfloat16)
    lead = jnp.dot(hits, lead_of, preferred_element_type=jnp.float32)
    return jnp.where(hit, base + rank, -1.0), lead


def fill_queries(cand_ref, q_ref):
    lane = lax.broadcasted_iota(jnp.int32, (CANDS, WIDTH), 1)
    pick = lax.broadcasted_iota(jnp.int32, (ROWS, WIDTH), 1)

    def one(u, carry):
        cand = cand_ref[u]
        column = u // 2 * 32 + lax.rem(u, 2)
        bias = jnp.where(pick == column, 1.0, 0.0).astype(jnp.bfloat16)
        for h in range(HEADS):
            q_ref[u, h, CANDS:ROWS, 0:WIDTH] = jnp.zeros((ROWS - CANDS, WIDTH), jnp.bfloat16)
            q_ref[u, h, 0:CANDS, 0:WIDTH] = jnp.where(lane // 32 == h, cand, jnp.zeros_like(cand))
            q_ref[u, h, :, WIDTH:] = bias
        return carry

    lax.fori_loop(0, OWN, one, 0)


def bias_columns(lead):
    r = lax.broadcasted_iota(jnp.int32, (SLOTS, PER_CHUNK), 0)
    b = lax.broadcasted_iota(jnp.int32, (SLOTS, PER_CHUNK), 1)
    repeat = jnp.where(r // CAP == b, 1.0, 0.0).astype(jnp.bfloat16)
    lead = jnp.dot(repeat, lead.astype(jnp.bfloat16), preferred_element_type=jnp.float32)
    slot = lax.rem(lax.broadcasted_iota(jnp.int32, (SLOTS, WIDTH), 0), CAP).astype(jnp.float32)
    follow = lax.rem(lax.broadcasted_iota(jnp.int32, (SLOTS, WIDTH), 1), 2)
    mine = jnp.where(follow == 1, slot - lead, lead - slot - 1.0) >= 0.0
    return jnp.where(mine, 0.0, -1e30).astype(jnp.bfloat16)


def pair_step(p, keys, bias, q_ref, m_ref, num_ref, den_ref):
    lane = lax.broadcasted_iota(jnp.int32, (SLOTS, WIDTH), 1)
    out_lane = lax.broadcasted_iota(jnp.int32, (ROWS, WIDTH), 1)
    key_ext = jnp.concatenate([keys, bias], axis=1)
    values = []
    for h in range(HEADS):
        own = lane // 32 == h
        ones = jnp.where(own, 1.0, 0.0).astype(jnp.bfloat16)
        values.append(jnp.concatenate([jnp.where(own, keys, jnp.zeros_like(keys)), ones], axis=1))
    for v in range(2):
        u = p * 2 + v
        total = None
        alpha = None
        for h in range(HEADS):
            s = lax.dot_general(q_ref[u, h], key_ext, (((1,), (1,)), ((), ())),
                                preferred_element_type=jnp.float32) * SCALE
            old = m_ref[u, h]
            new = jnp.maximum(old, jnp.max(s, axis=1, keepdims=True))
            m_ref[u, h] = new
            weights = jnp.exp2(s - jnp.concatenate([new, new], axis=1)).astype(jnp.bfloat16)
            part = jnp.dot(weights, values[h], preferred_element_type=jnp.float32)
            total = part if total is None else total + part
            shrink = jnp.exp2(old - new)
            alpha = shrink if alpha is None else jnp.where(out_lane // 32 == h, shrink, alpha)
        num_ref[u] = num_ref[u] * alpha + total[:, :WIDTH]
        den_ref[u] = den_ref[u] * alpha + total[:, WIDTH:]


def fused_kernel(hist_hbm, cats_ref, cand_cat_ref, cand_ref, out_ref,
                 hist_ref, id_row_ref, ids_ref, key_ref, cnt_ref, send_ref, cnt_in_ref, recv_ref,
                 q_ref, m_ref, num_ref, den_ref, bias_ref,
                 hist_sems, line_send, line_recv, plane_send, plane_recv,
                 cnt_send, cnt_recv, data_send, data_recv):
    at = place()
    role, y, z, x = at
    base = y * 16 + z * 4
    me = role * 64 + base + x
    line, plane = line_peers(at), plane_peers(at)

    barrier = pltpu.get_barrier_semaphore()
    for r, s in plane + line:
        signal(barrier, r, s)
    loads = [
        pltpu.make_async_copy(hist_hbm.at[e], hist_ref.at[:, pl.ds(e * OWN, OWN), :], hist_sems.at[e])
        for e in range(E_DEV)
    ]
    for load in loads:
        load.start()
    id_row_ref[...] = distinct_row(cand_cat_ref[...].astype(jnp.float32))
    pl.semaphore_wait(barrier, len(line) + len(plane))

    for r, s in line:
        push(id_row_ref, ids_ref.at[pl.ds(me, 1)], line_send, line_recv, r, s)
    pltpu.make_async_copy(id_row_ref, ids_ref.at[pl.ds(me, 1)], line_recv).start()
    fill_queries(cand_ref, q_ref)
    landed(ids_ref.at[pl.ds(0, 8)], line_recv)
    for r, s in plane:
        for half in range(2):
            rows = ids_ref.at[pl.ds(half * 64 + base, 4)]
            push(rows, rows, plane_send, plane_recv, r, s)
    m_ref[...] = jnp.full_like(m_ref, -3e38)
    num_ref[...] = jnp.zeros_like(num_ref)
    den_ref[...] = jnp.zeros_like(den_ref)
    landed(ids_ref.at[pl.ds(0, 120)], plane_recv)

    key_ref[...], cnt_ref[...] = matched(ids_ref[...], cats_ref[...])
    for load in loads:
        load.wait()
    rows = lax.broadcasted_iota(jnp.int32, (PAIRS * CAP, LANES), 0).astype(jnp.float32)

    def data_step(block, carry):
        peers = [partner(block, k, at) for k in range(BLOCK)]
        first = block * BLOCK
        chunk = block // (PER_CHUNK // BLOCK)
        for k, (r, s) in enumerate(peers):
            t = r * 64 + s
            pick = jnp.where(key_ref[pl.ds(t, 1), :] == rows, 1.0, 0.0).astype(jnp.bfloat16)
            packed = jnp.dot(pick, hist_ref[t], preferred_element_type=jnp.float32)
            send_ref[first + k] = packed.astype(jnp.bfloat16).reshape(PAIRS, CAP, WIDTH)
        for k, (r, s) in enumerate(peers):
            i = first + k
            cnt_src, cnt_dst = cnt_ref.at[pl.ds(r * 64 + s, 1)], cnt_in_ref.at[pl.ds(i, 1)]
            src, dst = send_ref.at[i], recv_ref.at[:, pl.ds(pl.multiple_of(i * CAP, CAP), CAP), :]

            def away(r=r, s=s, cnt_src=cnt_src, cnt_dst=cnt_dst, src=src, dst=dst):
                push(cnt_src, cnt_dst, cnt_send, cnt_recv.at[chunk], r, s)
                push(src, dst, data_send, data_recv.at[chunk], r, s)

            if k < BLOCK - 1:
                away()
            else:
                last = block == DEVS // BLOCK - 1
                pl.when(jnp.logical_not(last))(away)

                @pl.when(last)
                def _(cnt_src=cnt_src, cnt_dst=cnt_dst, src=src, dst=dst):
                    pltpu.make_async_copy(cnt_src, cnt_dst, cnt_recv.at[chunk]).start()
                    pltpu.make_async_copy(src, dst, data_recv.at[chunk]).start()
        return carry

    lax.fori_loop(0, DEVS // BLOCK, data_step, 0)

    def chunk_step(c, carry):
        counts = cnt_in_ref.at[pl.ds(c * PER_CHUNK, PER_CHUNK)]
        landed(counts, cnt_recv.at[c])
        slots = pl.ds(pl.multiple_of(c * SLOTS, SLOTS), SLOTS)
        landed(recv_ref.at[:, slots, :], data_recv.at[c])
        bias_ref[...] = bias_columns(counts[...])

        def one(p, carry):
            pair_step(p, recv_ref[p, slots, :], bias_ref[...], q_ref, m_ref, num_ref, den_ref)
            return carry

        return lax.fori_loop(0, PAIRS, one, carry)

    lax.fori_loop(0, CHUNKS, chunk_step, 0)

    def finish(u, carry):
        out_ref[u] = (num_ref[u, 0:CANDS, :] / den_ref[u, 0:CANDS, :]).astype(jnp.bfloat16)
        return carry

    lax.fori_loop(0, OWN, finish, 0)

    others = pl.ds(0, DEVS - 1)
    landed(send_ref.at[others], data_send)
    landed(cnt_ref.at[others], cnt_send)
    landed(ids_ref.at[pl.ds(0, 7)], line_send)
    landed(ids_ref.at[pl.ds(0, 120)], plane_send)


def interest_of(history, event_cat, candidates, cand_cat):
    hist = history.transpose(1, 0, 2).reshape(E_DEV, DEVS, OWN, WIDTH)
    cats = event_cat.astype(jnp.float32).T.reshape(E_DEV, DEVS, OWN).transpose(1, 0, 2).reshape(DEVS, LANES)
    vm = pl.BlockSpec(memory_space=pltpu.VMEM)
    f32, bf16 = jnp.float32, jnp.bfloat16
    return pl.pallas_call(
        fused_kernel,
        out_shape=jax.ShapeDtypeStruct((OWN, CANDS, WIDTH), bf16),
        in_specs=[pl.BlockSpec(memory_space=pl.ANY), vm, vm, vm],
        out_specs=vm,
        scratch_shapes=[
            pltpu.VMEM((DEVS, LANES, WIDTH), bf16),
            pltpu.VMEM((1, WIDTH), f32),
            pltpu.VMEM((DEVS, WIDTH), f32),
            pltpu.VMEM((DEVS, LANES), f32),
            pltpu.VMEM((DEVS, WIDTH), f32),
            pltpu.VMEM((DEVS, PAIRS, CAP, WIDTH), bf16),
            pltpu.VMEM((DEVS, WIDTH), f32),
            pltpu.VMEM((PAIRS, DEVS * CAP, WIDTH), bf16),
            pltpu.VMEM((OWN, HEADS, ROWS, 2 * WIDTH), bf16),
            pltpu.VMEM((OWN, HEADS, ROWS, WIDTH), f32),
            pltpu.VMEM((OWN, ROWS, WIDTH), f32),
            pltpu.VMEM((OWN, ROWS, WIDTH), f32),
            pltpu.VMEM((SLOTS, WIDTH), bf16),
            pltpu.SemaphoreType.DMA((E_DEV,)),
            pltpu.SemaphoreType.DMA, pltpu.SemaphoreType.DMA, pltpu.SemaphoreType.DMA, pltpu.SemaphoreType.DMA,
            pltpu.SemaphoreType.DMA, pltpu.SemaphoreType.DMA((CHUNKS,)),
            pltpu.SemaphoreType.DMA, pltpu.SemaphoreType.DMA((CHUNKS,)),
        ],
        compiler_params=pltpu.CompilerParams(collective_id=0, has_side_effects=True,
                                             vmem_limit_bytes=56 << 20),
        name="match_and_attend",
    )(hist, cats, cand_cat, candidates)


def local(history, event_cat, candidates, cand_cat, w_input, w_output):
    interest = interest_of(history, event_cat, candidates, cand_cat)
    rows = OWN * CANDS
    hidden = jnp.dot(candidates.reshape(rows, WIDTH), w_input[:WIDTH], preferred_element_type=jnp.float32)
    hidden += jnp.dot(interest.reshape(rows, WIDTH), w_input[WIDTH:], preferred_element_type=jnp.float32)
    hidden = jax.nn.silu(hidden).astype(jnp.bfloat16)
    result = jnp.dot(hidden, w_output, preferred_element_type=jnp.float32).astype(jnp.bfloat16)
    return result.reshape(OWN, CANDS, WIDTH)


def solution(mesh):
    return jax.shard_map(
        local, mesh=mesh,
        in_specs=(P(None, AXES, None), P(None, AXES), P(AXES, None, None), P(AXES, None), P(), P()),
        out_specs=P(AXES, None, None), check_vma=False)
```

time: 83.2 us -> 56.5 us (0.68)
  the two profiles are of different devices: /device:TPU:1 before, /device:TPU:8 now
where the time goes in v2:
time: 56.5 us; the launch traced here: 56.3 us
  Pallas kernels  49.4 us (87%)
  matrix products  4.76 us (8%)
  local copies, waits for them, and re-layouts  1.21 us (2%)
  other arithmetic  0.94 us (2%)
    pallas_call x1, Pallas kernels, interest_of(): pl.pallas_call(fused_kernel, out_shape=jax.ShapeDtypeStruct((OWN, CANDS,...  49.4 us
    dot_general x1, matrix products, local(): jnp.dot(hidden, w_output, preferred_element_type=jnp.float32)  3.17 us
    dot_general x1, matrix products, local(): jnp.dot(candidates.reshape(rows, WIDTH), w_input[:WIDTH], preferred_eleme...  1.59 us

profile of v2, /device:TPU:8, one launch (start us, length us, event | category | flops | bytes accessed | tf_op | source)
XLA Modules:
  0.0 56.3 jit_solution(5094832063369697171)
XLA Ops:
  0.0 0.0 copy-start
  0.0 0.9 %convert_bitcast_fusion = f32[20,1024]{1,0:T(8,128)S(1)} fusion(s32[1024,20]{0,1:T(8,128)} %param.7), kind=kLoop, calls=%fused_computation.6 | loop fusion | flops 20480 | bytes 163840 | tf_op jit(solution)/shard_map/transpose | solution.py:281
  0.9 0.2 copy.8
  1.2 0.2 copy.9
  1.4 0.8 %copy.10.cats_ref = f32[128,160]{1,0:T(8,128)} copy(f32[128,160]{0,1:T(8,128)S(1)} %bitcast.19) | data formatting | bytes 163840 | tf_op jit(solution)/shard_map/reshape | solution.py:281
  2.2 49.4 %match_and_attend.1 = bf16[8,200,128]{2,1,0:T(8,128)(2,1)} custom-call(bf16[20,128,8,128]{3,2,1,0:T(8,128)(2,1)} %bitcast.15, f32[128,160]{1,0:T(8,128)} %copy.10.cats_ref, s32[8,200]{1,0:T(8,128)} %cand_cat_ref.1, bf16[8,200,128]{2,1,0:T(8,128)(2,1)} %cand_ref.1), custom_call_target="tpu_custom_call" | custom-call | tf_op jit(solution)/shard_map/match_and_attend/pallas_call | solution.py:284
  51.5 1.6 %fusion.2 = f32[1600,512]{1,0:T(8,128)S(1)} fusion(bf16[1600,128]{1,0:T(8,128)(2,1)} %bitcast.17, bf16[256,512]{1,0:T(8,128)(2,1)} %param.10), kind=kOutput, calls=%fused_computation.4 | convolution fusion | flops 209715200 | bytes 3817472 | tf_op jit(solution)/shard_map/dot_general | solution.py:317
  53.1 0.0 copy-done
  53.1 3.2 %convolution_convert_fusion = bf16[1600,128]{1,0:T(8,128)(2,1)} fusion(bf16[512,128]{1,0:T(8,128)(2,1)S(1)} %copy-done, f32[1600,512]{1,0:T(8,128)S(1)} %fusion.2, bf16[1600,128]{1,0:T(8,128)(2,1)} %bitcast.18, bf16[256,512]{1,0:T(8,128)(2,1)} %param.10), kind=kOutput, calls=%fused_computation.2 | convolution fusion | flops 424550400 | bytes 4358144 | tf_op jit(solution)/shard_map/dot_general | solution.py:320
Async XLA Ops:
  0.0 53.1 %copy-start = (bf16[512,128]{1,0:T(8,128)(2,1)S(1)}, bf16[512,128]{1,0:T(8,128)(2,1)}, u32[]{:S(2)}) copy-start(bf16[512,128]{1,0:T(8,128)(2,1)} %param.11) | copy-start | bytes 393220

commit v3 on v2

--- a/solution.py
+++ b/solution.py
@@ -23,6 +23,7 @@
 CANDS = 200
 ROWS = 208
 HEADS = 4
+HID = 512
 CHUNKS = 4
 PER_CHUNK = DEVS // CHUNKS
 SLOTS = PER_CHUNK * CAP
@@ -31,11 +32,6 @@
 FAR = (2, 3, 1, 0)
 
 
-def far(k):
-    late = k // 2
-    return (2 + k) * (1 - late) + (3 - k) * late
-
-
 def place():
     role = lax.axis_index("role")
     shard = lax.axis_index("shard")
@@ -44,11 +40,10 @@
 
 def partner(block, k, at):
     role, y, z, x = at
-    r = lax.rem(role + 1 - k % 2, 2)
-    px = lax.rem(x + FAR[(k // 2) % 4], 4)
-    pz = lax.rem(z + far(lax.rem(block, 2) * 2 + k // 8), 4)
-    py = lax.rem(y + far(block // 2), 4)
-    return r, py * 16 + pz * 4 + px
+    r = lax.rem(role + 1 - lax.rem(block, 2), 2)
+    dy, dz = FAR[k // 4], FAR[k % 4]
+    px = lax.rem(x + block // 2 + 1 + 8 - dy - dz, 4)
+    return r, lax.rem(y + dy, 4) * 16 + lax.rem(z + dz, 4) * 4 + px
 
 
 def signal(sem, r, s):
@@ -90,6 +85,24 @@
     low = lax.rem(row, 32)
     lane1 = lax.broadcasted_iota(jnp.int32, (1, WIDTH), 1)
     return jnp.where(lane1 < 64, row - low, low).astype(jnp.float32)
+
+
+def flat_events(cats_ref, pad_ref, cols_ref):
+    pad_ref[...] = jnp.zeros_like(pad_ref)
+    pad_ref[0:E_DEV, :] = cats_ref[...]
+    for j in range(OWN):
+        cols_ref[j * WIDTH:(j + 1) * WIDTH, 0:32] = pad_ref[:, j * WIDTH:(j + 1) * WIDTH].T
+    e = lax.broadcasted_iota(jnp.int32, (32, LANES), 0)
+    lane = lax.broadcasted_iota(jnp.int32, (32, LANES), 1)
+    flat = None
+    for u in range(OWN):
+        value = cols_ref[pl.ds(u, DEVS, stride=OWN), 0:32]
+        low = lax.rem(value, 32)
+        spot = jnp.where(lane == e * OWN + u, 1.0, 0.0).astype(jnp.bfloat16)
+        for part in (value - low, low):
+            moved = jnp.dot(part.astype(jnp.float32).astype(jnp.bfloat16), spot, preferred_element_type=jnp.float32)
+            flat = moved if flat is None else flat + moved
+    return flat
 
 
 def matched(ids, events):
@@ -174,8 +187,8 @@
         den_ref[u] = den_ref[u] * alpha + total[:, WIDTH:]
 
 
-def fused_kernel(hist_hbm, cats_ref, cand_cat_ref, cand_ref, out_ref,
-                 hist_ref, id_row_ref, ids_ref, key_ref, cnt_ref, send_ref, cnt_in_ref, recv_ref,
+def fused_kernel(hist_hbm, cats_ref, cand_cat_ref, cand_ref, w_in_ref, w_out_ref, out_ref,
+                 pad_ref, cols_ref, events_ref, hid_ref, hist_ref, id_row_ref, ids_ref, key_ref, cnt_ref, send_ref, cnt_in_ref, recv_ref,
                  q_ref, m_ref, num_ref, den_ref, bias_ref,
                  hist_sems, line_send, line_recv, plane_send, plane_recv,
                  cnt_send, cnt_recv, data_send, data_recv):
@@ -200,6 +213,7 @@
     for r, s in line:
         push(id_row_ref, ids_ref.at[pl.ds(me, 1)], line_send, line_recv, r, s)
     pltpu.make_async_copy(id_row_ref, ids_ref.at[pl.ds(me, 1)], line_recv).start()
+    events_ref[...] = flat_events(cats_ref, pad_ref, cols_ref)
     fill_queries(cand_ref, q_ref)
     landed(ids_ref.at[pl.ds(0, 8)], line_recv)
     for r, s in plane:
@@ -209,9 +223,15 @@
     m_ref[...] = jnp.full_like(m_ref, -3e38)
     num_ref[...] = jnp.zeros_like(num_ref)
     den_ref[...] = jnp.zeros_like(den_ref)
+
+    def candidate_part(u, carry):
+        hid_ref[u] = jnp.dot(cand_ref[u], w_in_ref[0:WIDTH, :], preferred_element_type=jnp.float32)
+        return carry
+
+    lax.fori_loop(0, OWN, candidate_part, 0)
     landed(ids_ref.at[pl.ds(0, 120)], plane_recv)
 
-    key_ref[...], cnt_ref[...] = matched(ids_ref[...], cats_ref[...])
+    key_ref[...], cnt_ref[...] = matched(ids_ref[...], events_ref[...])
     for load in loads:
         load.wait()
     rows = lax.broadcasted_iota(jnp.int32, (PAIRS * CAP, LANES), 0).astype(jnp.float32)
@@ -264,7 +284,10 @@
     lax.fori_loop(0, CHUNKS, chunk_step, 0)
 
     def finish(u, carry):
-        out_ref[u] = (num_ref[u, 0:CANDS, :] / den_ref[u, 0:CANDS, :]).astype(jnp.bfloat16)
+        interest = (num_ref[u, 0:CANDS, :] / den_ref[u, 0:CANDS, :]).astype(jnp.bfloat16)
+        hidden = hid_ref[u] + jnp.dot(interest, w_in_ref[WIDTH:, :], preferred_element_type=jnp.float32)
+        hidden = (hidden / (1.0 + jnp.exp(-hidden))).astype(jnp.bfloat16)
+        out_ref[u] = jnp.dot(hidden, w_out_ref[...], preferred_element_type=jnp.float32).astype(jnp.bfloat16)
         return carry
 
     lax.fori_loop(0, OWN, finish, 0)
@@ -276,17 +299,20 @@
     landed(ids_ref.at[pl.ds(0, 120)], plane_send)
 
 
-def interest_of(history, event_cat, candidates, cand_cat):
+def local(history, event_cat, candidates, cand_cat, w_input, w_output):
     hist = history.transpose(1, 0, 2).reshape(E_DEV, DEVS, OWN, WIDTH)
-    cats = event_cat.astype(jnp.float32).T.reshape(E_DEV, DEVS, OWN).transpose(1, 0, 2).reshape(DEVS, LANES)
     vm = pl.BlockSpec(memory_space=pltpu.VMEM)
     f32, bf16 = jnp.float32, jnp.bfloat16
     return pl.pallas_call(
         fused_kernel,
         out_shape=jax.ShapeDtypeStruct((OWN, CANDS, WIDTH), bf16),
-        in_specs=[pl.BlockSpec(memory_space=pl.ANY), vm, vm, vm],
+        in_specs=[pl.BlockSpec(memory_space=pl.ANY), vm, vm, vm, vm, vm],
         out_specs=vm,
         scratch_shapes=[
+            pltpu.VMEM((32, DEVS * OWN), jnp.int32),
+            pltpu.VMEM((DEVS * OWN, WIDTH), jnp.int32),
+            pltpu.VMEM((DEVS, LANES), f32),
+            pltpu.VMEM((OWN, CANDS, HID), f32),
             pltpu.VMEM((DEVS, LANES, WIDTH), bf16),
             pltpu.VMEM((1, WIDTH), f32),
             pltpu.VMEM((DEVS, WIDTH), f32),
@@ -308,17 +334,7 @@
         compiler_params=pltpu.CompilerParams(collective_id=0, has_side_effects=True,
                                              vmem_limit_bytes=56 << 20),
         name="match_and_attend",
-    )(hist, cats, cand_cat, candidates)
-
-
-def local(history, event_cat, candidates, cand_cat, w_input, w_output):
-    interest = interest_of(history, event_cat, candidates, cand_cat)
-    rows = OWN * CANDS
-    hidden = jnp.dot(candidates.reshape(rows, WIDTH), w_input[:WIDTH], preferred_element_type=jnp.float32)
-    hidden += jnp.dot(interest.reshape(rows, WIDTH), w_input[WIDTH:], preferred_element_type=jnp.float32)
-    hidden = jax.nn.silu(hidden).astype(jnp.bfloat16)
-    result = jnp.dot(hidden, w_output, preferred_element_type=jnp.float32).astype(jnp.bfloat16)
-    return result.reshape(OWN, CANDS, WIDTH)
+    )(hist, event_cat.T, cand_cat, candidates, w_input, w_output)
 
 
 def solution(mesh):

time: 56.5 us -> 48.4 us (0.86)
  the two profiles are of different devices: /device:TPU:8 before, /device:TPU:0 now
where the time goes in v3:
time: 48.4 us; the launch traced here: 48.3 us
  Pallas kernels  46.5 us (96%)
  local copies, waits for them, and re-layouts  1.78 us (4%)
    pallas_call x1, Pallas kernels, local(): pl.pallas_call(fused_kernel, out_shape=jax.ShapeDtypeStruct((OWN, CANDS,...  46.5 us
    unnamed x1, local copies, waits for them, and re-layouts  1.78 us

profile of v3, /device:TPU:0, one launch (start us, length us, event | category | flops | bytes accessed | tf_op | source)
XLA Modules:
  0.0 48.3 jit_solution(8257874398160864835)
XLA Ops:
  0.0 46.5 %match_and_attend.1 = bf16[8,200,128]{2,1,0:T(8,128)(2,1)} custom-call(bf16[20,128,8,128]{3,2,1,0:T(8,128)(2,1)} %bitcast.4, s32[20,1024]{1,0:T(8,128)} %bitcast.5, s32[8,200]{1,0:T(8,128)} %cand_cat_ref.1, bf16[8,200,128]{2,1,0:T(8,128)(2,1)} %cand_ref.1, bf16[256,512]{1,0:T(8,128)(2,1)} %w_in_ref.1, bf16[512,128]{1,0:T(8,128)(2,1)} %w_out_ref.1), custom_call_target="tpu_custom_call" | custom-call | tf_op jit(solution)/shard_map/match_and_attend/pallas_call | solution.py:306
  46.5 1.8 %copy.8 = bf16[8,200,128]{2,1,0:T(8,128)(2,1)} copy(bf16[8,200,128]{2,1,0:T(8,128)(2,1)} %match_and_attend.1) | data formatting | bytes 819200

commit v4 on v3

--- a/solution.py
+++ b/solution.py
@@ -24,6 +24,9 @@
 ROWS = 208
 HEADS = 4
 HID = 512
+HEAD = WIDTH // HEADS
+USER = HEADS * ROWS
+COLS = 2 * USER
 CHUNKS = 4
 PER_CHUNK = DEVS // CHUNKS
 SLOTS = PER_CHUNK * CAP
@@ -132,66 +135,88 @@
 
 
 def fill_queries(cand_ref, q_ref):
-    lane = lax.broadcasted_iota(jnp.int32, (CANDS, WIDTH), 1)
-    pick = lax.broadcasted_iota(jnp.int32, (ROWS, WIDTH), 1)
-
-    def one(u, carry):
-        cand = cand_ref[u]
-        column = u // 2 * 32 + lax.rem(u, 2)
-        bias = jnp.where(pick == column, 1.0, 0.0).astype(jnp.bfloat16)
-        for h in range(HEADS):
-            q_ref[u, h, CANDS:ROWS, 0:WIDTH] = jnp.zeros((ROWS - CANDS, WIDTH), jnp.bfloat16)
-            q_ref[u, h, 0:CANDS, 0:WIDTH] = jnp.where(lane // 32 == h, cand, jnp.zeros_like(cand))
-            q_ref[u, h, :, WIDTH:] = bias
+    row = lax.broadcasted_iota(jnp.int32, (WIDTH, ROWS), 0)
+
+    def one(p, carry):
+        parts = []
+        for v in range(2):
+            cand = cand_ref[p * 2 + v].astype(jnp.float32)
+            cand = jnp.concatenate([cand, jnp.zeros((256 - CANDS, WIDTH), jnp.float32)], axis=0)
+            turned = cand.T[:, :ROWS]
+            for h in range(HEADS):
+                parts.append(jnp.where(row // HEAD == h, turned, 0.0))
+        q_ref[p] = jnp.concatenate(parts, axis=1).astype(jnp.bfloat16)
         return carry
 
-    lax.fori_loop(0, OWN, one, 0)
-
-
-def bias_columns(lead):
+    lax.fori_loop(0, PAIRS, one, 0)
+
+
+def fill_owners(lead, mask_ref):
+    a = lax.broadcasted_iota(jnp.int32, (WIDTH, PAIRS * WIDTH), 0)
+    b = lax.broadcasted_iota(jnp.int32, (WIDTH, PAIRS * WIDTH), 1)
+    wide = jnp.dot(lead.astype(jnp.bfloat16), jnp.where(a == b // WIDTH * 32, 1.0, 0.0).astype(jnp.bfloat16),
+                   preferred_element_type=jnp.float32)
     r = lax.broadcasted_iota(jnp.int32, (SLOTS, PER_CHUNK), 0)
-    b = lax.broadcasted_iota(jnp.int32, (SLOTS, PER_CHUNK), 1)
-    repeat = jnp.where(r // CAP == b, 1.0, 0.0).astype(jnp.bfloat16)
-    lead = jnp.dot(repeat, lead.astype(jnp.bfloat16), preferred_element_type=jnp.float32)
+    c = lax.broadcasted_iota(jnp.int32, (SLOTS, PER_CHUNK), 1)
+    tall = jnp.dot(jnp.where(r // CAP == c, 1.0, 0.0).astype(jnp.bfloat16), wide.astype(jnp.bfloat16),
+                   preferred_element_type=jnp.float32)
     slot = lax.rem(lax.broadcasted_iota(jnp.int32, (SLOTS, WIDTH), 0), CAP).astype(jnp.float32)
-    follow = lax.rem(lax.broadcasted_iota(jnp.int32, (SLOTS, WIDTH), 1), 2)
-    mine = jnp.where(follow == 1, slot - lead, lead - slot - 1.0) >= 0.0
-    return jnp.where(mine, 0.0, -1e30).astype(jnp.bfloat16)
-
-
-def pair_step(p, keys, bias, q_ref, m_ref, num_ref, den_ref):
-    lane = lax.broadcasted_iota(jnp.int32, (SLOTS, WIDTH), 1)
-    out_lane = lax.broadcasted_iota(jnp.int32, (ROWS, WIDTH), 1)
-    key_ext = jnp.concatenate([keys, bias], axis=1)
-    values = []
-    for h in range(HEADS):
-        own = lane // 32 == h
-        ones = jnp.where(own, 1.0, 0.0).astype(jnp.bfloat16)
-        values.append(jnp.concatenate([jnp.where(own, keys, jnp.zeros_like(keys)), ones], axis=1))
-    for v in range(2):
-        u = p * 2 + v
-        total = None
-        alpha = None
-        for h in range(HEADS):
-            s = lax.dot_general(q_ref[u, h], key_ext, (((1,), (1,)), ((), ())),
-                                preferred_element_type=jnp.float32) * SCALE
-            old = m_ref[u, h]
-            new = jnp.maximum(old, jnp.max(s, axis=1, keepdims=True))
-            m_ref[u, h] = new
-            weights = jnp.exp2(s - jnp.concatenate([new, new], axis=1)).astype(jnp.bfloat16)
-            part = jnp.dot(weights, values[h], preferred_element_type=jnp.float32)
-            total = part if total is None else total + part
-            shrink = jnp.exp2(old - new)
-            alpha = shrink if alpha is None else jnp.where(out_lane // 32 == h, shrink, alpha)
-        num_ref[u] = num_ref[u] * alpha + total[:, :WIDTH]
-        den_ref[u] = den_ref[u] * alpha + total[:, WIDTH:]
-
-
-def fused_kernel(hist_hbm, cats_ref, cand_cat_ref, cand_ref, w_in_ref, w_out_ref, out_ref,
-                 pad_ref, cols_ref, events_ref, hid_ref, hist_ref, id_row_ref, ids_ref, key_ref, cnt_ref, send_ref, cnt_in_ref, recv_ref,
-                 q_ref, m_ref, num_ref, den_ref, bias_ref,
-                 hist_sems, line_send, line_recv, plane_send, plane_recv,
-                 cnt_send, cnt_recv, data_send, data_recv):
+    first = lax.broadcasted_iota(jnp.int32, (SLOTS, WIDTH), 1) < USER % WIDTH
+    for p in range(PAIRS):
+        one = jnp.where(slot < tall[:, p * WIDTH:(p + 1) * WIDTH], 1.0, 0.0)
+        for i, kind in enumerate((one, jnp.where(first, one, 1.0 - one), 1.0 - one)):
+            mask_ref[p, i] = kind.astype(mask_ref.dtype)
+
+
+def by_tile(ref, p):
+    whole = USER // WIDTH
+    return jnp.concatenate([ref[p, 0]] * whole + [ref[p, 1]] + [ref[p, 2]] * whole, axis=1)
+
+
+def value_rows(keys):
+    turned = keys.astype(jnp.float32).T.astype(jnp.bfloat16)
+    return jnp.concatenate([turned, jnp.ones((16, SLOTS), jnp.bfloat16)], axis=0)
+
+
+def own_head(o):
+    tiles = []
+    for lo in range(0, COLS, WIDTH):
+        h0, h1 = lo % USER // ROWS, (lo + WIDTH - 1) % USER // ROWS
+        tile = o[HEAD * h0:HEAD * (h0 + 1), lo:lo + WIDTH]
+        if h1 != h0:
+            lane = lax.broadcasted_iota(jnp.int32, (HEAD, WIDTH), 1)
+            tile = jnp.where(lane < ROWS - lo % ROWS, tile, o[HEAD * h1:HEAD * (h1 + 1), lo:lo + WIDTH])
+        tiles.append(tile)
+    return jnp.concatenate(tiles, axis=1)
+
+
+def plain_step(p, keys, mask_ref, q_ref, acc_ref):
+    s = jnp.dot(keys, q_ref[p], preferred_element_type=jnp.float32) * SCALE
+    weights = jnp.exp2(s).astype(jnp.bfloat16) * by_tile(mask_ref, p)
+    o = jnp.dot(value_rows(keys), weights, preferred_element_type=jnp.float32)
+    acc_ref[p, 0:HEAD, :] += own_head(o)
+    acc_ref[p, HEAD:, :] += o[WIDTH:WIDTH + 8]
+
+
+def shifted_step(p, keys, mask_ref, q_ref, top_ref, acc_ref):
+    s = jnp.dot(keys, q_ref[p], preferred_element_type=jnp.float32) * SCALE
+    s = jnp.where(by_tile(mask_ref, p) > 0.5, s, -1e30)
+    old = top_ref[p]
+    new = jnp.maximum(old, jnp.max(s, axis=0, keepdims=True))
+    top_ref[p] = new
+    shrink = jnp.exp2(old - new)
+    weights = jnp.exp2(s - new).astype(jnp.bfloat16)
+    o = jnp.dot(value_rows(keys), weights, preferred_element_type=jnp.float32)
+    acc_ref[p, 0:HEAD, :] = acc_ref[p, 0:HEAD, :] * shrink + own_head(o)
+    acc_ref[p, HEAD:, :] = acc_ref[p, HEAD:, :] * shrink + o[WIDTH:WIDTH + 8]
+
+
+def exchange_kernel(hist_hbm, cats_hbm, cand_cat_hbm, cand_hbm, acc_ref, recv_ref, cnt_in_ref,
+                    cats_ref, cand_cat_ref, cand_ref,
+                    pad_ref, cols_ref, events_ref, hist_ref, id_row_ref, ids_ref, key_ref, cnt_ref, send_ref,
+                    q_ref, mask_ref,
+                    small_sems, hist_sems, line_send, line_recv, plane_send, plane_recv,
+                    cnt_send, cnt_recv, data_send, data_recv):
     at = place()
     role, y, z, x = at
     base = y * 16 + z * 4
@@ -201,34 +226,36 @@
     barrier = pltpu.get_barrier_semaphore()
     for r, s in plane + line:
         signal(barrier, r, s)
+    smalls = [
+        pltpu.make_async_copy(src, dst, small_sems.at[n])
+        for n, (src, dst) in enumerate((
+            (cand_cat_hbm, cand_cat_ref), (cats_hbm, cats_ref), (cand_hbm, cand_ref)))
+    ]
+    for small in smalls:
+        small.start()
     loads = [
         pltpu.make_async_copy(hist_hbm.at[e], hist_ref.at[:, pl.ds(e * OWN, OWN), :], hist_sems.at[e])
         for e in range(E_DEV)
     ]
     for load in loads:
         load.start()
+    smalls[0].wait()
     id_row_ref[...] = distinct_row(cand_cat_ref[...].astype(jnp.float32))
     pl.semaphore_wait(barrier, len(line) + len(plane))
 
     for r, s in line:
         push(id_row_ref, ids_ref.at[pl.ds(me, 1)], line_send, line_recv, r, s)
     pltpu.make_async_copy(id_row_ref, ids_ref.at[pl.ds(me, 1)], line_recv).start()
+    smalls[1].wait()
     events_ref[...] = flat_events(cats_ref, pad_ref, cols_ref)
+    smalls[2].wait()
     fill_queries(cand_ref, q_ref)
     landed(ids_ref.at[pl.ds(0, 8)], line_recv)
     for r, s in plane:
         for half in range(2):
             rows = ids_ref.at[pl.ds(half * 64 + base, 4)]
             push(rows, rows, plane_send, plane_recv, r, s)
-    m_ref[...] = jnp.full_like(m_ref, -3e38)
-    num_ref[...] = jnp.zeros_like(num_ref)
-    den_ref[...] = jnp.zeros_like(den_ref)
-
-    def candidate_part(u, carry):
-        hid_ref[u] = jnp.dot(cand_ref[u], w_in_ref[0:WIDTH, :], preferred_element_type=jnp.float32)
-        return carry
-
-    lax.fori_loop(0, OWN, candidate_part, 0)
+    acc_ref[...] = jnp.zeros_like(acc_ref)
     landed(ids_ref.at[pl.ds(0, 120)], plane_recv)
 
     key_ref[...], cnt_ref[...] = matched(ids_ref[...], events_ref[...])
@@ -273,24 +300,12 @@
         landed(counts, cnt_recv.at[c])
         slots = pl.ds(pl.multiple_of(c * SLOTS, SLOTS), SLOTS)
         landed(recv_ref.at[:, slots, :], data_recv.at[c])
-        bias_ref[...] = bias_columns(counts[...])
-
-        def one(p, carry):
-            pair_step(p, recv_ref[p, slots, :], bias_ref[...], q_ref, m_ref, num_ref, den_ref)
-            return carry
-
-        return lax.fori_loop(0, PAIRS, one, carry)
+        fill_owners(counts[...], mask_ref)
+        for p in range(PAIRS):
+            plain_step(p, recv_ref[p, slots, :], mask_ref, q_ref, acc_ref)
+        return carry
 
     lax.fori_loop(0, CHUNKS, chunk_step, 0)
-
-    def finish(u, carry):
-        interest = (num_ref[u, 0:CANDS, :] / den_ref[u, 0:CANDS, :]).astype(jnp.bfloat16)
-        hidden = hid_ref[u] + jnp.dot(interest, w_in_ref[WIDTH:, :], preferred_element_type=jnp.float32)
-        hidden = (hidden / (1.0 + jnp.exp(-hidden))).astype(jnp.bfloat16)
-        out_ref[u] = jnp.dot(hidden, w_out_ref[...], preferred_element_type=jnp.float32).astype(jnp.bfloat16)
-        return carry
-
-    lax.fori_loop(0, OWN, finish, 0)
 
     others = pl.ds(0, DEVS - 1)
     landed(send_ref.at[others], data_send)
@@ -299,42 +314,109 @@
     landed(ids_ref.at[pl.ds(0, 120)], plane_send)
 
 
+def finish(sums_ref, cand_ref, w_in_ref, w_out_ref, stage_ref, out_hbm, sems):
+    copies = []
+    for p in range(PAIRS):
+        share = sums_ref[p, 0:HEAD, :] * (1.0 / sums_ref[p, HEAD:HEAD + 1, :])
+        turned = jnp.concatenate([share[:, lo:lo + WIDTH].T for lo in range(0, COLS, WIDTH)], axis=0)
+        for v in range(2):
+            u = p * 2 + v
+            starts = [v * USER + h * ROWS for h in range(HEADS)]
+            interest = jnp.concatenate([turned[lo:lo + ROWS] for lo in starts], axis=1)[0:CANDS]
+            rows = jnp.concatenate([cand_ref[u], interest.astype(jnp.bfloat16)], axis=1)
+            hidden = jnp.dot(rows, w_in_ref[...], preferred_element_type=jnp.float32)
+            half = hidden * 0.5
+            hidden = (half + half * jnp.tanh(half)).astype(jnp.bfloat16)
+            stage_ref[u] = jnp.dot(hidden, w_out_ref[...], preferred_element_type=jnp.float32).astype(jnp.bfloat16)
+        both = pl.ds(p * 2, 2)
+        copies.append(pltpu.make_async_copy(stage_ref.at[both], out_hbm.at[both], sems.at[p]))
+        copies[-1].start()
+    for copy in copies:
+        copy.wait()
+
+
+def tower_kernel(acc_ref, cnt_ref, cand_ref, w_in_ref, w_out_ref, recv_hbm, out_hbm,
+                 stage_ref, again_ref, recv_ref, q_ref, mask_ref, top_ref, sems):
+    weights = acc_ref[:, HEAD:HEAD + 1, :]
+    good = (weights > 2.0 ** -80) & (weights < 2.0 ** 110)
+    safe = jnp.min(jnp.where(good, 1.0, 0.0)) > 0.5
+
+    @pl.when(safe)
+    def _():
+        finish(acc_ref, cand_ref, w_in_ref, w_out_ref, stage_ref, out_hbm, sems)
+
+    @pl.when(jnp.logical_not(safe))
+    def _():
+        pltpu.sync_copy(recv_hbm, recv_ref)
+        fill_queries(cand_ref, q_ref)
+        top_ref[...] = jnp.full_like(top_ref, -3e38)
+        again_ref[...] = jnp.zeros_like(again_ref)
+
+        def chunk_step(c, carry):
+            fill_owners(cnt_ref[pl.ds(pl.multiple_of(c * PER_CHUNK, PER_CHUNK), PER_CHUNK), :], mask_ref)
+
+            def one(p, carry):
+                keys = recv_ref[p, pl.ds(pl.multiple_of(c * SLOTS, SLOTS), SLOTS), :]
+                shifted_step(p, keys, mask_ref, q_ref, top_ref, again_ref)
+                return carry
+
+            return lax.fori_loop(0, PAIRS, one, carry)
+
+        lax.fori_loop(0, CHUNKS, chunk_step, 0)
+        finish(again_ref, cand_ref, w_in_ref, w_out_ref, stage_ref, out_hbm, sems)
+
+
 def local(history, event_cat, candidates, cand_cat, w_input, w_output):
     hist = history.transpose(1, 0, 2).reshape(E_DEV, DEVS, OWN, WIDTH)
     vm = pl.BlockSpec(memory_space=pltpu.VMEM)
-    f32, bf16 = jnp.float32, jnp.bfloat16
-    return pl.pallas_call(
-        fused_kernel,
-        out_shape=jax.ShapeDtypeStruct((OWN, CANDS, WIDTH), bf16),
-        in_specs=[pl.BlockSpec(memory_space=pl.ANY), vm, vm, vm, vm, vm],
-        out_specs=vm,
+    hbm = pl.BlockSpec(memory_space=pltpu.HBM)
+    f32, bf16, dma = jnp.float32, jnp.bfloat16, pltpu.SemaphoreType.DMA
+    sums, slots, counts = pl.pallas_call(
+        exchange_kernel,
+        out_shape=(
+            jax.ShapeDtypeStruct((PAIRS, HEAD + 8, COLS), f32),
+            jax.ShapeDtypeStruct((PAIRS, DEVS * CAP, WIDTH), bf16),
+            jax.ShapeDtypeStruct((DEVS, WIDTH), f32),
+        ),
+        in_specs=[hbm] * 4,
+        out_specs=(vm, vm, vm),
         scratch_shapes=[
+            pltpu.VMEM((E_DEV, DEVS * OWN), jnp.int32),
+            pltpu.VMEM((OWN, CANDS), jnp.int32),
+            pltpu.VMEM((OWN, CANDS, WIDTH), bf16),
             pltpu.VMEM((32, DEVS * OWN), jnp.int32),
             pltpu.VMEM((DEVS * OWN, WIDTH), jnp.int32),
             pltpu.VMEM((DEVS, LANES), f32),
-            pltpu.VMEM((OWN, CANDS, HID), f32),
             pltpu.VMEM((DEVS, LANES, WIDTH), bf16),
             pltpu.VMEM((1, WIDTH), f32),
             pltpu.VMEM((DEVS, WIDTH), f32),
             pltpu.VMEM((DEVS, LANES), f32),
             pltpu.VMEM((DEVS, WIDTH), f32),
             pltpu.VMEM((DEVS, PAIRS, CAP, WIDTH), bf16),
-            pltpu.VMEM((DEVS, WIDTH), f32),
+            pltpu.VMEM((PAIRS, WIDTH, COLS), bf16),
+            pltpu.VMEM((PAIRS, 3, SLOTS, WIDTH), bf16),
+            dma((3,)), dma((E_DEV,)), dma, dma, dma, dma, dma, dma((CHUNKS,)), dma, dma((CHUNKS,)),
+        ],
+        compiler_params=pltpu.CompilerParams(collective_id=0, has_side_effects=True, vmem_limit_bytes=40 << 20),
+        name="match_and_attend",
+    )(*(pltpu.with_memory_space_constraint(x, pltpu.HBM) for x in (hist, event_cat.T, cand_cat, candidates)))
+    return pl.pallas_call(
+        tower_kernel,
+        out_shape=jax.ShapeDtypeStruct((OWN, CANDS, WIDTH), bf16),
+        in_specs=[vm] * 5 + [pl.BlockSpec(memory_space=pl.ANY)],
+        out_specs=hbm,
+        scratch_shapes=[
+            pltpu.VMEM((OWN, CANDS, WIDTH), bf16),
+            pltpu.VMEM((PAIRS, HEAD + 8, COLS), f32),
             pltpu.VMEM((PAIRS, DEVS * CAP, WIDTH), bf16),
-            pltpu.VMEM((OWN, HEADS, ROWS, 2 * WIDTH), bf16),
-            pltpu.VMEM((OWN, HEADS, ROWS, WIDTH), f32),
-            pltpu.VMEM((OWN, ROWS, WIDTH), f32),
-            pltpu.VMEM((OWN, ROWS, WIDTH), f32),
-            pltpu.VMEM((SLOTS, WIDTH), bf16),
-            pltpu.SemaphoreType.DMA((E_DEV,)),
-            pltpu.SemaphoreType.DMA, pltpu.SemaphoreType.DMA, pltpu.SemaphoreType.DMA, pltpu.SemaphoreType.DMA,
-            pltpu.SemaphoreType.DMA, pltpu.SemaphoreType.DMA((CHUNKS,)),
-            pltpu.SemaphoreType.DMA, pltpu.SemaphoreType.DMA((CHUNKS,)),
+            pltpu.VMEM((PAIRS, WIDTH, COLS), bf16),
+            pltpu.VMEM((PAIRS, 3, SLOTS, WIDTH), f32),
+            pltpu.VMEM((PAIRS, 1, COLS), f32),
+            dma((PAIRS,)),
         ],
-        compiler_params=pltpu.CompilerParams(collective_id=0, has_side_effects=True,
-                                             vmem_limit_bytes=56 << 20),
-        name="match_and_attend",
-    )(hist, event_cat.T, cand_cat, candidates, w_input, w_output)
+        compiler_params=pltpu.CompilerParams(vmem_limit_bytes=40 << 20),
+        name="tower",
+    )(sums, counts, candidates, w_input, w_output, slots)
 
 
 def solution(mesh):

time: 48.4 us -> 55.7 us (1.15)
  the two profiles are of different devices: /device:TPU:0 before, /device:TPU:2 now
where the time goes in v4:
time: 55.7 us; the launch traced here: 55.3 us
  Pallas kernels  55.2 us (99%)
    pallas_call x1, Pallas kernels, local(): pl.pallas_call(exchange_kernel, out_shape=(jax.ShapeDtypeStruct((PAIRS, H...  34.2 us
    pallas_call x1, Pallas kernels, local(): pl.pallas_call(tower_kernel, out_shape=jax.ShapeDtypeStruct((OWN, CANDS,...  21 us

profile of v4, /device:TPU:2, one launch (start us, length us, event | category | flops | bytes accessed | tf_op | source)
XLA Modules:
  0.0 55.3 jit_solution(9635871006757703476)
XLA Ops:
  0.0 0.0 copy-start
  0.0 0.0 copy-start.2
  0.0 0.0 copy-start.1
  0.0 34.2 %match_and_attend.1 = (f32[4,40,1664]{2,1,0:T(8,128)S(1)}, bf16[4,1024,128]{2,1,0:T(8,128)(2,1)S(1)}, f32[128,128]{1,0:T(8,128)S(1)}) custom-call(bf16[20,128,8,128]{3,2,1,0:T(8,128)(2,1)} %bitcast.4, s32[20,1024]{1,0:T(8,128)} %bitcast.5, s32[8,200]{1,0:T(8,128)} %cand_cat_hbm.1, bf16[8,200,128]{2,1,0:T(8,128)(2,1)} %cand_ref.1), custom_call_target="tpu_custom_call" | custom-call | tf_op jit(solution)/shard_map/match_and_attend/pallas_call | solution.py:374
  34.2 0.0 copy-done
  34.2 0.0 copy-done.2
  34.2 0.0 copy-done.1
  34.3 21.0 %tower.1 = bf16[8,200,128]{2,1,0:T(8,128)(2,1)} custom-call(f32[4,40,1664]{2,1,0:T(8,128)S(1)} %get-tuple-element.8.acc_ref, f32[128,128]{1,0:T(8,128)S(1)} %get-tuple-element.9.cnt_ref, bf16[8,200,128]{2,1,0:T(8,128)(2,1)S(1)} %copy-done, bf16[256,512]{1,0:T(8,128)(2,1)S(1)} %copy-done.1, bf16[512,128]{1,0:T(8,128)(2,1)S(1)} %copy-done.2, ...), custom_call_target="tpu_custom_call" | custom-call | tf_op jit(solution)/shard_map/tower/pallas_call | solution.py:403
Async XLA Ops:
  0.0 34.2 %copy-start = (bf16[8,200,128]{2,1,0:T(8,128)(2,1)S(1)}, bf16[8,200,128]{2,1,0:T(8,128)(2,1)}, u32[]{:S(2)}) copy-start(bf16[8,200,128]{2,1,0:T(8,128)(2,1)} %cand_ref.1) | copy-start | bytes 1228804
  0.0 34.2 %copy-start.2 = (bf16[512,128]{1,0:T(8,128)(2,1)S(1)}, bf16[512,128]{1,0:T(8,128)(2,1)}, u32[]{:S(2)}) copy-start(bf16[512,128]{1,0:T(8,128)(2,1)} %w_out_ref.1) | copy-start | bytes 393220
  0.0 34.2 %copy-start.1 = (bf16[256,512]{1,0:T(8,128)(2,1)S(1)}, bf16[256,512]{1,0:T(8,128)(2,1)}, u32[]{:S(2)}) copy-start(bf16[256,512]{1,0:T(8,128)(2,1)} %w_in_ref.1) | copy-start | bytes 786436

commit v5 on v4

--- a/solution.py
+++ b/solution.py
@@ -108,28 +108,32 @@
     return flat
 
 
-def matched(ids, events):
+def matching_tables():
+    er = lax.broadcasted_iota(jnp.int32, (WIDTH, LANES), 0)
+    ec = lax.broadcasted_iota(jnp.int32, (WIDTH, LANES), 1)
+    expand = lax.rem(er, 8) == lax.rem(ec, 8)
+    a = lax.broadcasted_iota(jnp.int32, (LANES, LANES), 0)
+    b = lax.broadcasted_iota(jnp.int32, (LANES, LANES), 1)
+    ua, ub = lax.rem(a, 8), lax.rem(b, 8)
+    before = ((ua == ub) & (a < b)) | ((ua + 1 == ub) & (lax.rem(ub, 2) == 1))
+    ca = lax.broadcasted_iota(jnp.int32, (LANES, WIDTH), 0)
+    cb = lax.broadcasted_iota(jnp.int32, (LANES, WIDTH), 1)
+    lead_of = lax.rem(ca, 8) == cb // 32 * 2
+    return [jnp.where(table, 1.0, 0.0).astype(jnp.bfloat16) for table in (expand, before, lead_of)]
+
+
+def matched(ids, events, expand, before, lead_of):
     ids = ids.astype(jnp.bfloat16)
     lane_i = lax.broadcasted_iota(jnp.int32, (DEVS, WIDTH), 1)
-    er = lax.broadcasted_iota(jnp.int32, (WIDTH, LANES), 0)
-    ec = lax.broadcasted_iota(jnp.int32, (WIDTH, LANES), 1)
-    expand = jnp.where(lax.rem(er, 8) == lax.rem(ec, 8), 1.0, 0.0).astype(jnp.bfloat16)
     hit = None
     for k in range(QCAT):
         only = jnp.where(lax.rem(lane_i // 8, 8) == k, ids, jnp.zeros_like(ids))
         same = events == jnp.dot(only, expand, preferred_element_type=jnp.float32)
         hit = same if hit is None else hit | same
     hits = jnp.where(hit, 1.0, 0.0).astype(jnp.bfloat16)
-    a = lax.broadcasted_iota(jnp.int32, (LANES, LANES), 0)
-    b = lax.broadcasted_iota(jnp.int32, (LANES, LANES), 1)
-    ua, ub = lax.rem(a, 8), lax.rem(b, 8)
-    before = ((ua == ub) & (a < b)) | ((ua + 1 == ub) & (lax.rem(ub, 2) == 1))
-    rank = jnp.dot(hits, jnp.where(before, 1.0, 0.0).astype(jnp.bfloat16), preferred_element_type=jnp.float32)
+    rank = jnp.dot(hits, before, preferred_element_type=jnp.float32)
     lane_k = lax.broadcasted_iota(jnp.int32, (DEVS, LANES), 1)
     base = (lax.rem(lane_k, 8) // 2 * CAP).astype(jnp.float32)
-    ca = lax.broadcasted_iota(jnp.int32, (LANES, WIDTH), 0)
-    cb = lax.broadcasted_iota(jnp.int32, (LANES, WIDTH), 1)
-    lead_of = jnp.where(lax.rem(ca, 8) == cb // 32 * 2, 1.0, 0.0).astype(jnp.bfloat16)
     lead = jnp.dot(hits, lead_of, preferred_element_type=jnp.float32)
     return jnp.where(hit, base + rank, -1.0), lead
 
@@ -211,10 +215,10 @@
     acc_ref[p, HEAD:, :] = acc_ref[p, HEAD:, :] * shrink + o[WIDTH:WIDTH + 8]
 
 
-def exchange_kernel(hist_hbm, cats_hbm, cand_cat_hbm, cand_hbm, acc_ref, recv_ref, cnt_in_ref,
-                    cats_ref, cand_cat_ref, cand_ref,
+def exchange_kernel(hist_hbm, cats_hbm, cand_cat_hbm, cand_hbm, w_in_hbm, acc_ref, recv_ref, cnt_in_ref, hid_ref,
+                    cats_ref, cand_cat_ref, cand_ref, w_in_ref,
                     pad_ref, cols_ref, events_ref, hist_ref, id_row_ref, ids_ref, key_ref, cnt_ref, send_ref,
-                    q_ref, mask_ref,
+                    q_ref, mask_ref, expand_ref, before_ref, lead_of_ref,
                     small_sems, hist_sems, line_send, line_recv, plane_send, plane_recv,
                     cnt_send, cnt_recv, data_send, data_recv):
     at = place()
@@ -229,7 +233,8 @@
     smalls = [
         pltpu.make_async_copy(src, dst, small_sems.at[n])
         for n, (src, dst) in enumerate((
-            (cand_cat_hbm, cand_cat_ref), (cats_hbm, cats_ref), (cand_hbm, cand_ref)))
+            (cand_cat_hbm, cand_cat_ref), (cats_hbm, cats_ref), (cand_hbm, cand_ref),
+            (w_in_hbm.at[pl.ds(0, WIDTH)], w_in_ref)))
     ]
     for small in smalls:
         small.start()
@@ -256,11 +261,19 @@
             rows = ids_ref.at[pl.ds(half * 64 + base, 4)]
             push(rows, rows, plane_send, plane_recv, r, s)
     acc_ref[...] = jnp.zeros_like(acc_ref)
-    landed(ids_ref.at[pl.ds(0, 120)], plane_recv)
-
-    key_ref[...], cnt_ref[...] = matched(ids_ref[...], events_ref[...])
+    expand_ref[...], before_ref[...], lead_of_ref[...] = matching_tables()
+    smalls[3].wait()
+
+    def candidate_part(u, carry):
+        hid_ref[u, 0:CANDS, :] = jnp.dot(cand_ref[u], w_in_ref[...], preferred_element_type=jnp.float32)
+        return carry
+
+    lax.fori_loop(0, OWN, candidate_part, 0)
     for load in loads:
         load.wait()
+    landed(ids_ref.at[pl.ds(0, 120)], plane_recv)
+
+    key_ref[...], cnt_ref[...] = matched(ids_ref[...], events_ref[...], expand_ref[...], before_ref[...], lead_of_ref[...])
     rows = lax.broadcasted_iota(jnp.int32, (PAIRS * CAP, LANES), 0).astype(jnp.float32)
 
     def data_step(block, carry):
@@ -299,8 +312,8 @@
         counts = cnt_in_ref.at[pl.ds(c * PER_CHUNK, PER_CHUNK)]
         landed(counts, cnt_recv.at[c])
         slots = pl.ds(pl.multiple_of(c * SLOTS, SLOTS), SLOTS)
+        fill_owners(counts[...], mask_ref)
         landed(recv_ref.at[:, slots, :], data_recv.at[c])
-        fill_owners(counts[...], mask_ref)
         for p in range(PAIRS):
             plain_step(p, recv_ref[p, slots, :], mask_ref, q_ref, acc_ref)
         return carry
@@ -314,40 +327,39 @@
     landed(ids_ref.at[pl.ds(0, 120)], plane_send)
 
 
-def finish(sums_ref, cand_ref, w_in_ref, w_out_ref, stage_ref, out_hbm, sems):
+def finish(sums_ref, hid_ref, w_in_ref, w_out_ref, stage_ref, out_hbm, sems):
     copies = []
     for p in range(PAIRS):
         share = sums_ref[p, 0:HEAD, :] * (1.0 / sums_ref[p, HEAD:HEAD + 1, :])
         turned = jnp.concatenate([share[:, lo:lo + WIDTH].T for lo in range(0, COLS, WIDTH)], axis=0)
+        users = []
         for v in range(2):
-            u = p * 2 + v
             starts = [v * USER + h * ROWS for h in range(HEADS)]
-            interest = jnp.concatenate([turned[lo:lo + ROWS] for lo in starts], axis=1)[0:CANDS]
-            rows = jnp.concatenate([cand_ref[u], interest.astype(jnp.bfloat16)], axis=1)
-            hidden = jnp.dot(rows, w_in_ref[...], preferred_element_type=jnp.float32)
-            half = hidden * 0.5
-            hidden = (half + half * jnp.tanh(half)).astype(jnp.bfloat16)
-            stage_ref[u] = jnp.dot(hidden, w_out_ref[...], preferred_element_type=jnp.float32).astype(jnp.bfloat16)
+            users.append(jnp.concatenate([turned[lo:lo + ROWS] for lo in starts], axis=1))
+        interest = jnp.concatenate(users, axis=0).astype(jnp.bfloat16)
+        hidden = jnp.dot(interest, w_in_ref[WIDTH:, :], preferred_element_type=jnp.float32)
+        hidden = hidden + hid_ref[2 * p:2 * p + 2].reshape(2 * ROWS, HID)
+        half = hidden * 0.5
+        hidden = (half + half * jnp.tanh(half)).astype(jnp.bfloat16)
+        result = jnp.dot(hidden, w_out_ref[...], preferred_element_type=jnp.float32).astype(jnp.bfloat16)
+        stage_ref[2 * p:2 * p + 2] = result.reshape(2, ROWS, WIDTH)
         both = pl.ds(p * 2, 2)
-        copies.append(pltpu.make_async_copy(stage_ref.at[both], out_hbm.at[both], sems.at[p]))
+        copies.append(pltpu.make_async_copy(stage_ref.at[both, 0:CANDS], out_hbm.at[both], sems.at[p]))
         copies[-1].start()
     for copy in copies:
         copy.wait()
 
 
-def tower_kernel(acc_ref, cnt_ref, cand_ref, w_in_ref, w_out_ref, recv_hbm, out_hbm,
-                 stage_ref, again_ref, recv_ref, q_ref, mask_ref, top_ref, sems):
+def tower_kernel(acc_ref, cnt_ref, hid_ref, w_in_ref, w_out_ref, recv_hbm, cand_hbm, out_hbm,
+                 stage_ref, again_ref, recv_ref, cand_ref, q_ref, mask_ref, top_ref, sems):
+    finish(acc_ref, hid_ref, w_in_ref, w_out_ref, stage_ref, out_hbm, sems)
     weights = acc_ref[:, HEAD:HEAD + 1, :]
     good = (weights > 2.0 ** -80) & (weights < 2.0 ** 110)
-    safe = jnp.min(jnp.where(good, 1.0, 0.0)) > 0.5
-
-    @pl.when(safe)
-    def _():
-        finish(acc_ref, cand_ref, w_in_ref, w_out_ref, stage_ref, out_hbm, sems)
-
-    @pl.when(jnp.logical_not(safe))
+
+    @pl.when(jnp.min(jnp.where(good, 1.0, 0.0)) < 0.5)
     def _():
         pltpu.sync_copy(recv_hbm, recv_ref)
+        pltpu.sync_copy(cand_hbm, cand_ref)
         fill_queries(cand_ref, q_ref)
         top_ref[...] = jnp.full_like(top_ref, -3e38)
         again_ref[...] = jnp.zeros_like(again_ref)
@@ -363,7 +375,7 @@
             return lax.fori_loop(0, PAIRS, one, carry)
 
         lax.fori_loop(0, CHUNKS, chunk_step, 0)
-        finish(again_ref, cand_ref, w_in_ref, w_out_ref, stage_ref, out_hbm, sems)
+        finish(again_ref, hid_ref, w_in_ref, w_out_ref, stage_ref, out_hbm, sems)
 
 
 def local(history, event_cat, candidates, cand_cat, w_input, w_output):
@@ -371,19 +383,21 @@
     vm = pl.BlockSpec(memory_space=pltpu.VMEM)
     hbm = pl.BlockSpec(memory_space=pltpu.HBM)
     f32, bf16, dma = jnp.float32, jnp.bfloat16, pltpu.SemaphoreType.DMA
-    sums, slots, counts = pl.pallas_call(
+    sums, slots, counts, hidden = pl.pallas_call(
         exchange_kernel,
         out_shape=(
             jax.ShapeDtypeStruct((PAIRS, HEAD + 8, COLS), f32),
             jax.ShapeDtypeStruct((PAIRS, DEVS * CAP, WIDTH), bf16),
             jax.ShapeDtypeStruct((DEVS, WIDTH), f32),
+            jax.ShapeDtypeStruct((OWN, ROWS, HID), f32),
         ),
-        in_specs=[hbm] * 4,
-        out_specs=(vm, vm, vm),
+        in_specs=[hbm] * 5,
+        out_specs=(vm, vm, vm, vm),
         scratch_shapes=[
             pltpu.VMEM((E_DEV, DEVS * OWN), jnp.int32),
             pltpu.VMEM((OWN, CANDS), jnp.int32),
             pltpu.VMEM((OWN, CANDS, WIDTH), bf16),
+            pltpu.VMEM((WIDTH, HID), bf16),
             pltpu.VMEM((32, DEVS * OWN), jnp.int32),
             pltpu.VMEM((DEVS * OWN, WIDTH), jnp.int32),
             pltpu.VMEM((DEVS, LANES), f32),
@@ -395,20 +409,24 @@
             pltpu.VMEM((DEVS, PAIRS, CAP, WIDTH), bf16),
             pltpu.VMEM((PAIRS, WIDTH, COLS), bf16),
             pltpu.VMEM((PAIRS, 3, SLOTS, WIDTH), bf16),
-            dma((3,)), dma((E_DEV,)), dma, dma, dma, dma, dma, dma((CHUNKS,)), dma, dma((CHUNKS,)),
+            pltpu.VMEM((WIDTH, LANES), bf16),
+            pltpu.VMEM((LANES, LANES), bf16),
+            pltpu.VMEM((LANES, WIDTH), bf16),
+            dma((4,)), dma((E_DEV,)), dma, dma, dma, dma, dma, dma((CHUNKS,)), dma, dma((CHUNKS,)),
         ],
         compiler_params=pltpu.CompilerParams(collective_id=0, has_side_effects=True, vmem_limit_bytes=40 << 20),
         name="match_and_attend",
-    )(*(pltpu.with_memory_space_constraint(x, pltpu.HBM) for x in (hist, event_cat.T, cand_cat, candidates)))
+    )(*(pltpu.with_memory_space_constraint(x, pltpu.HBM) for x in (hist, event_cat.T, cand_cat, candidates, w_input)))
     return pl.pallas_call(
         tower_kernel,
         out_shape=jax.ShapeDtypeStruct((OWN, CANDS, WIDTH), bf16),
-        in_specs=[vm] * 5 + [pl.BlockSpec(memory_space=pl.ANY)],
+        in_specs=[vm] * 5 + [pl.BlockSpec(memory_space=pl.ANY)] * 2,
         out_specs=hbm,
         scratch_shapes=[
-            pltpu.VMEM((OWN, CANDS, WIDTH), bf16),
+            pltpu.VMEM((OWN, ROWS, WIDTH), bf16),
             pltpu.VMEM((PAIRS, HEAD + 8, COLS), f32),
             pltpu.VMEM((PAIRS, DEVS * CAP, WIDTH), bf16),
+            pltpu.VMEM((OWN, CANDS, WIDTH), bf16),
             pltpu.VMEM((PAIRS, WIDTH, COLS), bf16),
             pltpu.VMEM((PAIRS, 3, SLOTS, WIDTH), f32),
             pltpu.VMEM((PAIRS, 1, COLS), f32),
@@ -416,7 +434,7 @@
         ],
         compiler_params=pltpu.CompilerParams(vmem_limit_bytes=40 << 20),
         name="tower",
-    )(sums, counts, candidates, w_input, w_output, slots)
+    )(sums, counts, hidden, w_input, w_output, slots, candidates)
 
 
 def solution(mesh):

time: 55.7 us -> 57.9 us (1.039)
  the two profiles are of different devices: /device:TPU:2 before, /device:TPU:1 now
where the time goes in v5:
time: 57.9 us; the launch traced here: 57.5 us
  Pallas kernels  57.5 us (99%)
    pallas_call x1, Pallas kernels, local(): pl.pallas_call(exchange_kernel, out_shape=(jax.ShapeDtypeStruct((PAIRS, H...  34.5 us
    pallas_call x1, Pallas kernels, local(): pl.pallas_call(tower_kernel, out_shape=jax.ShapeDtypeStruct((OWN, CANDS,...  23 us

profile of v5, /device:TPU:1, one launch (start us, length us, event | category | flops | bytes accessed | tf_op | source)
XLA Modules:
  0.0 57.5 jit_solution(14724442370679579177)
XLA Ops:
  0.0 0.0 copy-start.1
  0.0 0.0 copy-start
  0.0 0.0 copy-start.2
  0.0 34.5 %match_and_attend.1 = (f32[4,40,1664]{2,1,0:T(8,128)S(1)}, bf16[4,1024,128]{2,1,0:T(8,128)(2,1)S(1)}, f32[128,128]{1,0:T(8,128)S(1)}, f32[8,208,512]{2,1,0:T(8,128)S(1)}) custom-call(bf16[20,128,8,128]{3,2,1,0:T(8,128)(2,1)} %bitcast.4, s32[20,1024]{1,0:T(8,128)} %bitcast.5, s32[8,200]{1,0:T(8,128)} %cand_cat_hbm.1, bf16[8,200,128]{2,1,0:T(8,128)(2,1)} %cand_hbm.3, ...), custom_call_target="tpu_custom_call" | custom-call | tf_op jit(solution)/shard_map/match_and_attend/pallas_call | solution.py:386
  34.5 0.0 copy-done.1
  34.5 0.0 copy-done
  34.5 0.0 copy-done.2
  34.6 23.0 %tower.1 = bf16[8,200,128]{2,1,0:T(8,128)(2,1)} custom-call(f32[4,40,1664]{2,1,0:T(8,128)S(1)} %get-tuple-element.9.acc_ref, f32[128,128]{1,0:T(8,128)S(1)} %get-tuple-element.10.cnt_ref, f32[8,208,512]{2,1,0:T(8,128)S(1)} %get-tuple-element.11.hid_ref, bf16[256,512]{1,0:T(8,128)(2,1)S(1)} %copy-done.1, bf16[512,128]{1,0:T(8,128)(2,1)S(1)} %copy-done.2, ...), custom_call_target="tpu_custom_call" | custom-call | tf_op jit(solution)/shard_map/tower/pallas_call | solution.py:420
Async XLA Ops:
  0.0 34.5 %copy-start.1 = (bf16[256,512]{1,0:T(8,128)(2,1)S(1)}, bf16[256,512]{1,0:T(8,128)(2,1)}, u32[]{:S(2)}) copy-start(bf16[256,512]{1,0:T(8,128)(2,1)} %w_in_ref.1) | copy-start | bytes 786436
  0.0 34.5 %copy-start = (bf16[8,200,128]{2,1,0:T(8,128)(2,1)S(1)}, bf16[8,200,128]{2,1,0:T(8,128)(2,1)}, u32[]{:S(2)}) copy-start(bf16[8,200,128]{2,1,0:T(8,128)(2,1)} %cand_hbm.3) | copy-start | bytes 1228804
  0.0 34.5 %copy-start.2 = (bf16[512,128]{1,0:T(8,128)(2,1)S(1)}, bf16[512,128]{1,0:T(8,128)(2,1)}, u32[]{:S(2)}) copy-start(bf16[512,128]{1,0:T(8,128)(2,1)} %w_out_ref.1) | copy-start | bytes 393220

commit v6 on v5

--- a/solution.py
+++ b/solution.py
@@ -331,11 +331,12 @@
     copies = []
     for p in range(PAIRS):
         share = sums_ref[p, 0:HEAD, :] * (1.0 / sums_ref[p, HEAD:HEAD + 1, :])
-        turned = jnp.concatenate([share[:, lo:lo + WIDTH].T for lo in range(0, COLS, WIDTH)], axis=0)
         users = []
         for v in range(2):
             starts = [v * USER + h * ROWS for h in range(HEADS)]
-            users.append(jnp.concatenate([turned[lo:lo + ROWS] for lo in starts], axis=1))
+            tall = jnp.concatenate([share[:, lo:lo + ROWS] for lo in starts], axis=0)
+            tall = jnp.concatenate([tall, jnp.zeros((WIDTH, 2 * WIDTH - ROWS), jnp.float32)], axis=1)
+            users.append(tall.T[0:ROWS])
         interest = jnp.concatenate(users, axis=0).astype(jnp.bfloat16)
         hidden = jnp.dot(interest, w_in_ref[WIDTH:, :], preferred_element_type=jnp.float32)
         hidden = hidden + hid_ref[2 * p:2 * p + 2].reshape(2 * ROWS, HID)

time: 57.9 us -> 56.9 us (0.983)
  the two profiles are of different devices: /device:TPU:1 before, /device:TPU:32 now
where the time goes in v6:
time: 56.9 us; the launch traced here: 56.2 us
  Pallas kernels  56.2 us (99%)
    pallas_call x1, Pallas kernels, local(): pl.pallas_call(exchange_kernel, out_shape=(jax.ShapeDtypeStruct((PAIRS, H...  33.8 us
    pallas_call x1, Pallas kernels, local(): pl.pallas_call(tower_kernel, out_shape=jax.ShapeDtypeStruct((OWN, CANDS,...  22.4 us

profile of v6, /device:TPU:32, one launch (start us, length us, event | category | flops | bytes accessed | tf_op | source)
XLA Modules:
  0.0 56.2 jit_solution(7379209565305176060)
XLA Ops:
  0.0 0.0 copy-start.1
  0.0 0.0 copy-start
  0.0 0.0 copy-start.2
  0.0 33.8 %match_and_attend.1 = (f32[4,40,1664]{2,1,0:T(8,128)S(1)}, bf16[4,1024,128]{2,1,0:T(8,128)(2,1)S(1)}, f32[128,128]{1,0:T(8,128)S(1)}, f32[8,208,512]{2,1,0:T(8,128)S(1)}) custom-call(bf16[20,128,8,128]{3,2,1,0:T(8,128)(2,1)} %bitcast.4, s32[20,1024]{1,0:T(8,128)} %bitcast.5, s32[8,200]{1,0:T(8,128)} %cand_cat_hbm.1, bf16[8,200,128]{2,1,0:T(8,128)(2,1)} %cand_hbm.3, ...), custom_call_target="tpu_custom_call" | custom-call | tf_op jit(solution)/shard_map/match_and_attend/pallas_call | solution.py:387
  33.8 0.0 copy-done.1
  33.8 0.0 copy-done
  33.8 0.0 copy-done.2
  33.8 22.4 %tower.1 = bf16[8,200,128]{2,1,0:T(8,128)(2,1)} custom-call(f32[4,40,1664]{2,1,0:T(8,128)S(1)} %get-tuple-element.9.acc_ref, f32[128,128]{1,0:T(8,128)S(1)} %get-tuple-element.10.cnt_ref, f32[8,208,512]{2,1,0:T(8,128)S(1)} %get-tuple-element.11.hid_ref, bf16[256,512]{1,0:T(8,128)(2,1)S(1)} %copy-done.1, bf16[512,128]{1,0:T(8,128)(2,1)S(1)} %copy-done.2, ...), custom_call_target="tpu_custom_call" | custom-call | tf_op jit(solution)/shard_map/tower/pallas_call | solution.py:421
Async XLA Ops:
  0.0 33.8 %copy-start.1 = (bf16[256,512]{1,0:T(8,128)(2,1)S(1)}, bf16[256,512]{1,0:T(8,128)(2,1)}, u32[]{:S(2)}) copy-start(bf16[256,512]{1,0:T(8,128)(2,1)} %w_in_ref.1) | copy-start | bytes 786436
  0.0 33.8 %copy-start = (bf16[8,200,128]{2,1,0:T(8,128)(2,1)S(1)}, bf16[8,200,128]{2,1,0:T(8,128)(2,1)}, u32[]{:S(2)}) copy-start(bf16[8,200,128]{2,1,0:T(8,128)(2,1)} %cand_hbm.3) | copy-start | bytes 1228804
  0.0 33.8 %copy-start.2 = (bf16[512,128]{1,0:T(8,128)(2,1)S(1)}, bf16[512,128]{1,0:T(8,128)(2,1)}, u32[]{:S(2)}) copy-start(bf16[512,128]{1,0:T(8,128)(2,1)} %w_out_ref.1) | copy-start | bytes 393220
